TPU v7x, 128 devices: a whole 4x4x4 slice. The times are simulated.
128 devices in a mesh: data: 1, expert: 128 (over z, y, x, core).
Axes of the slice: x: 4, y: 4, z: 4, core: 2. Of those that a mesh axis runs over, the one named last changes fastest.
Arguments:
- tokens: bfloat16 [16384, 2048], P(('data', 'expert'))
- expert_ids: int32 [16384, 8], P(('data', 'expert'))
- gate_wts: float32 [16384, 8], P(('data', 'expert'))
- dev_slot: int32 [16384, 8], P(('data', 'expert'))
- exp_slot: int32 [16384, 8], P(('data', 'expert'))
- w_gate: bfloat16 [128, 2048, 768], P('expert')
- w_up: bfloat16 [128, 2048, 768], P('expert')
- w_down: bfloat16 [128, 768, 2048], P('expert')
Outputs:
- output: bfloat16 [16384, 2048], P(('data', 'expert'))
All inputs are finite; a program needn't handle non-finite values.
Results may differ from a plain program's by a relative error of at most 0.00784482.
Values are sent between devices in bfloat16 or wider.
A program may use at most 1 GiB of HBM per device.

v0:
```python
import jax
import jax.numpy as jnp
from jax import lax
from jax.sharding import PartitionSpec as P, NamedSharding


def value_a10(tok_dev, top_k, groups, n_experts):
    dev_cap = min(tok_dev, 8 * ((3 * tok_dev * top_k + 16 * groups - 1) // (16 * groups)))
    exp_cap = 8 * ((tok_dev * groups * top_k + 4 * n_experts - 1) // (4 * n_experts))
    return dev_cap, exp_cap


def solution(mesh):
    groups = mesh.shape["expert"]
    row_spec = P(("data", "expert"), None)
    weight_spec = P("expert", None, None)

    def device_layer(tokens, expert_ids, gate_wts, dev_slot, exp_slot, w_gate, w_up, w_down):
        tok_dev, top_k = expert_ids.shape
        d_model = tokens.shape[1]
        e_local = w_gate.shape[0]
        dev_cap, exp_cap = value_a10(tok_dev, top_k, groups, e_local * groups)
        n_rows = groups * dev_cap
        kept_choice = (dev_slot >= 0) & (exp_slot >= 0)
        dest_row = jnp.where(kept_choice, (expert_ids // e_local) * dev_cap + dev_slot, -1)
        row_hit = jnp.arange(n_rows)[:, None, None] == dest_row[None, :, :]
        pick_mat = jnp.any(row_hit, axis=2).astype(jnp.bfloat16)
        send_x = jnp.dot(pick_mat, tokens, preferred_element_type=jnp.float32).astype(jnp.bfloat16)
        ex_hit = (expert_ids % e_local)[:, :, None] == jnp.arange(e_local)
        meta_vals = jnp.stack([gate_wts, (exp_slot + 1).astype(jnp.float32)], axis=-1)
        meta_in = jnp.where(ex_hit[:, :, :, None], meta_vals[:, :, None, :], 0.0)
        send_meta = jnp.einsum("rtk,tkec->rec", row_hit.astype(jnp.float32), meta_in, precision=lax.Precision.HIGHEST)
        recv_x = lax.all_to_all(send_x.reshape(groups, dev_cap, d_model), "expert", 0, 0, tiled=True)
        recv_meta = lax.all_to_all(send_meta.reshape(groups, dev_cap, e_local, 2), "expert", 0, 0, tiled=True)
        recv_x = recv_x.reshape(n_rows, d_model)
        recv_meta = recv_meta.reshape(n_rows, e_local, 2)
        slot_ids = jnp.arange(1, exp_cap + 1).astype(jnp.float32)
        gather_mat = (recv_meta[:, :, 1].T[:, None, :] == slot_ids[:, None]).astype(jnp.bfloat16)
        exp_in = jnp.einsum("esr,rd->esd", gather_mat, recv_x, preferred_element_type=jnp.float32).astype(jnp.bfloat16)
        hid_gate = jnp.einsum("esd,edf->esf", exp_in, w_gate, preferred_element_type=jnp.float32)
        hid_up = jnp.einsum("esd,edf->esf", exp_in, w_up, preferred_element_type=jnp.float32)
        hidden = (jax.nn.silu(hid_gate) * hid_up).astype(jnp.bfloat16)
        exp_out = jnp.einsum("esf,efd->esd", hidden, w_down, preferred_element_type=jnp.float32).astype(jnp.bfloat16)
        scatter_mat = gather_mat * recv_meta[:, :, 0].T.astype(jnp.bfloat16)[:, None, :]
        z_rows = jnp.einsum("esr,esd->rd", scatter_mat, exp_out, preferred_element_type=jnp.float32).astype(jnp.bfloat16)
        back_rows = lax.all_to_all(z_rows.reshape(groups, dev_cap, d_model), "expert", 0, 0, tiled=True)
        moe_out = jnp.einsum("rt,rd->td", pick_mat, back_rows.reshape(n_rows, d_model), preferred_element_type=jnp.float32)
        return moe_out.astype(jnp.bfloat16)

    def moe_layer(tokens, expert_ids, gate_wts, dev_slot, exp_slot, w_gate, w_up, w_down):
        mapped = jax.shard_map(device_layer, mesh=mesh, in_specs=(row_spec,) * 5 + (weight_spec,) * 3, out_specs=row_spec, check_vma=False)
        return mapped(tokens, expert_ids, gate_wts, dev_slot, exp_slot, w_gate, w_up, w_down)

    return moe_layer
```

profile of v0, /device:TPU:1, one launch (start us, length us, event | category | flops | bytes accessed | tf_op | source)
XLA Modules:
  0.0 341.0 jit_solution(2100127070714252835)
XLA Ops:
  0.0 0.0 copy-start
  0.0 0.9 add_convert_fusion.1
  0.9 4.3 %fusion.28 = f32[128,16,1,2]{0,3,1,2:T(2,128)S(1)} fusion(s32[8,128]{1,0:T(8,128)S(1)} %bitcast.51, s32[128,16]{0,1:T(8,128)S(1)} %multiply_add_fusion, f32[128,8,1]{0,2,1:T(1,128)S(1)} %bitcast.54, f32[128,8,1]{0,2,1:T(1,128)} %bitcast.55), kind=kOutput, calls=%fused_computation.27 | convolution fusion | flops 52430848 | bytes 36864 | tf_op jit(solution)/shard_map/rtk,tkec->rec/dot_general | solution.py:32
  5.2 0.8 copy.18
  6.0 11.5 %all-to-all-start = ((f32[128,16,1,2]{1,3,2,0:T(2,128)}), f32[128,16,1,2]{1,3,2,0:T(2,128)S(1)}, u32[]{:S(2)}, u32[]{:S(2)}) async-start(f32[128,16,1,2]{1,3,2,0:T(2,128)} %copy.18), calls=%async_computation | async-start | bytes 262144 | tf_op jit(solution)/shard_map/all_to_all | solution.py:34
  17.5 7.4 %fusion.10 = pred[2048,128]{1,0:T(8,128)(4,1)S(1)} fusion(s32[128,8]{0,1:T(8,128)S(1)} %get-tuple-element.6), kind=kLoop, calls=%fused_computation.11 | loop fusion | flops 3932160 | bytes 266240 | tf_op jit(solution)/shard_map/reduce_or | solution.py:27
  24.9 6.6 %convolution_convert_fusion = bf16[2048,2048]{1,0:T(8,128)(2,1)} fusion(pred[2048,128]{1,0:T(8,128)(4,1)S(1)} %fusion.10, bf16[128,2048]{1,0:T(8,128)(2,1)} %param.8), kind=kOutput, calls=%fused_computation.16 | convolution fusion | flops 1077936128 | bytes 9175040 | tf_op jit(solution)/shard_map/dot_general | solution.py:28
  31.5 0.0 all-to-all-done
  31.5 10.2 %all-to-all-start.1 = ((bf16[128,16,2048]{2,1,0:T(8,128)(2,1)}), bf16[128,16,2048]{2,1,0:T(8,128)(2,1)}, u32[]{:S(2)}, u32[]{:S(2)}) async-start(bf16[128,16,2048]{2,1,0:T(8,128)(2,1)} %bitcast.49), calls=%async_computation.1 | async-start | bytes 16777216 | tf_op jit(solution)/shard_map/all_to_all | solution.py:33
  41.8 0.7 copy.19
  42.5 1.0 reshape.138
  43.5 107.2 %all-to-all-done.1 = bf16[128,16,2048]{2,1,0:T(8,128)(2,1)} async-done(((bf16[128,16,2048]{2,1,0:T(8,128)(2,1)}), bf16[128,16,2048]{2,1,0:T(8,128)(2,1)}, u32[]{:S(2)}, u32[]{:S(2)}) %all-to-all-start.1) | async-done | bytes 8388640 | tf_op jit(solution)/shard_map/all_to_all | solution.py:33
  150.7 0.0 copy-start.1
  150.7 20.8 %fusion.16 = bf16[2048,2048]{1,0:T(8,128)(2,1)S(1)} fusion(bf16[2048,2048]{1,0:T(8,128)(2,1)} %bitcast.10, f32[2048]{0:T(1024)S(1)} %bitcast.52, f32[2048]{0:T(1024)S(1)} %add_convert_fusion), kind=kOutput, calls=%fused_computation.15 | convolution fusion | flops 17188257792 | bytes 16793600 | tf_op jit(solution)/shard_map/esr,rd->esd/dot_general | solution.py:39
  171.6 0.0 copy-done.1
  171.6 0.0 copy-start.2
  171.6 6.8 %fusion.26 = f32[2048,768]{1,0:T(8,128)S(1)} fusion(bf16[2048,2048]{1,0:T(8,128)(2,1)S(1)} %fusion.16, bf16[1,2048,768]{2,1,0:T(8,128)(2,1)S(1)} %copy-done.1), kind=kOutput, calls=%fused_computation.24 | convolution fusion | flops 6442450944 | bytes 17825792 | tf_op jit(solution)/shard_map/esd,edf->esf/dot_general | solution.py:40
  178.4 0.0 copy-done.2
  178.4 7.5 %multiply_convert_fusion = bf16[2048,768]{1,0:T(8,128)(2,1)S(1)} fusion(f32[2048,768]{1,0:T(8,128)S(1)} %fusion.26, bf16[2048,2048]{1,0:T(8,128)(2,1)S(1)} %fusion.16, bf16[1,2048,768]{2,1,0:T(8,128)(2,1)S(1)} %copy-done.2), kind=kOutput, calls=%fused_computation.17 | convolution fusion | flops 6451888128 | bytes 20971520 | tf_op jit(solution)/shard_map/esd,edf->esf/dot_general | solution.py:41
  186.0 0.0 copy-done
  186.0 7.1 %fusion.55 = bf16[2048,2048]{1,0:T(8,128)(2,1)S(1)} fusion(bf16[2048,768]{1,0:T(8,128)(2,1)S(1)} %multiply_convert_fusion, bf16[1,768,2048]{2,1,0:T(8,128)(2,1)S(1)} %copy-done), kind=kOutput, calls=%fused_computation.4.clone.clone.clone.2 | convolution fusion | flops 6446645248 | bytes 14680064 | tf_op jit(solution)/shard_map/esf,efd->esd/dot_general | solution.py:43
  193.1 20.1 %fusion.13 = bf16[2048,2048]{1,0:T(8,128)(2,1)S(1)} fusion(f32[2048]{0:T(1024)S(1)} %bitcast.53, f32[2048]{0:T(1024)S(1)} %add_convert_fusion, bf16[2048]{0:T(1024)(128)(2,1)S(1)} %fusion.31, bf16[2048,2048]{1,0:T(8,128)(2,1)S(1)} %fusion.55), kind=kOutput, calls=%fused_computation.14 | convolution fusion | flops 17192452096 | bytes 16797696 | tf_op jit(solution)/shard_map/esr,esd->rd/dot_general | solution.py:45
  213.2 125.7 %all_to_all.15 = bf16[128,16,2048]{2,1,0:T(8,128)(2,1)S(1)} all-to-all(bf16[128,16,2048]{2,1,0:T(8,128)(2,1)S(1)} %bitcast.50), channel_id=1, replica_groups=mesh['data'=1,'expert'=128] {'expert'}, dimensions={0} | all-to-all | bytes 16777216 | tf_op jit(solution)/shard_map/all_to_all | solution.py:46
  338.9 2.2 convolution_convert_fusion.1
  (4 shorter events, 0.1 us)
Async XLA Ops:
  0.0 186.0 %copy-start = (bf16[1,768,2048]{2,1,0:T(8,128)(2,1)S(1)}, bf16[1,768,2048]{2,1,0:T(8,128)(2,1)}, u32[]{:S(2)}) copy-start(bf16[1,768,2048]{2,1,0:T(8,128)(2,1)} %param.15) | copy-start | bytes 9437188
  6.0 25.5 %all-to-all-start = ((f32[128,16,1,2]{1,3,2,0:T(2,128)}), f32[128,16,1,2]{1,3,2,0:T(2,128)S(1)}, u32[]{:S(2)}, u32[]{:S(2)}) async-start(f32[128,16,1,2]{1,3,2,0:T(2,128)} %copy.18), calls=%async_computation | async-start | bytes 262144 | tf_op jit(solution)/shard_map/all_to_all | solution.py:34
  31.5 119.2 %all-to-all-start.1 = ((bf16[128,16,2048]{2,1,0:T(8,128)(2,1)}), bf16[128,16,2048]{2,1,0:T(8,128)(2,1)}, u32[]{:S(2)}, u32[]{:S(2)}) async-start(bf16[128,16,2048]{2,1,0:T(8,128)(2,1)} %bitcast.49), calls=%async_computation.1 | async-start | bytes 16777216 | tf_op jit(solution)/shard_map/all_to_all | solution.py:33
  150.7 20.9 %copy-start.1 = (bf16[1,2048,768]{2,1,0:T(8,128)(2,1)S(1)}, bf16[1,2048,768]{2,1,0:T(8,128)(2,1)}, u32[]{:S(2)}) copy-start(bf16[1,2048,768]{2,1,0:T(8,128)(2,1)} %param.13) | copy-start | bytes 9437188
  171.6 6.8 %copy-start.2 = (bf16[1,2048,768]{2,1,0:T(8,128)(2,1)S(1)}, bf16[1,2048,768]{2,1,0:T(8,128)(2,1)}, u32[]{:S(2)}) copy-start(bf16[1,2048,768]{2,1,0:T(8,128)(2,1)} %param.14) | copy-start | bytes 9437188
where the time goes:
time: 342 us; the launch traced here: 341 us
  blocking collectives  126 us (37%)
  waiting for transfers between devices  107 us (31%)
  matrix products  75.5 us (22%)
  starting transfers between devices  21.7 us (6%)
  other arithmetic  8.3 us (2%)
    all_to_all x1, blocking collectives, device_layer(): lax.all_to_all(z_rows.reshape(groups, dev_cap, d_model), 'expert', 0, 0,...  126 us
    all_to_all x1, waiting for transfers between devices, device_layer(): lax.all_to_all(send_x.reshape(groups, dev_cap, d_model), 'expert', 0, 0,...  107 us
    dot_general x1, matrix products, device_layer(): jnp.einsum('esr,rd->esd', gather_mat, recv_x, preferred_element_type=jnp....  20.8 us
    dot_general x1, matrix products, device_layer(): jnp.einsum('esr,esd->rd', scatter_mat, exp_out, preferred_element_type=jn...  20.1 us
    all_to_all x1, starting transfers between devices, device_layer(): lax.all_to_all(send_meta.reshape(groups, dev_cap, e_local, 2), 'expert',...  11.5 us
    all_to_all x1, starting transfers between devices, device_layer(): lax.all_to_all(send_x.reshape(groups, dev_cap, d_model), 'expert', 0, 0,...  10.2 us
    dot_general x1, matrix products, device_layer(): jnp.einsum('esd,edf->esf', exp_in, w_up, preferred_element_type=jnp.float32)  7.55 us
    reduce_or x1, other arithmetic, device_layer(): pick_mat = jnp.any(row_hit, axis=2).astype(jnp.bfloat16)  7.42 us
  transfers between devices with their start and end apart: 2, of which 1 were waited for; matrix products, arithmetic and copies ran while one was open for 5% of the time, Pallas kernels for 0%

commit v1 on v0

v1 whole, which is shorter than its diff:
```python
import jax
import jax.numpy as jnp
from jax import lax
from jax.sharding import PartitionSpec as P


def solution(mesh):
    groups = mesh.shape["expert"]
    row_spec = P(("data", "expert"), None)
    weight_spec = P("expert", None, None)

    def device_layer(tokens, expert_ids, gate_wts, dev_slot, exp_slot, w_gate, w_up, w_down):
        tok_dev, top_k = expert_ids.shape
        d_model = tokens.shape[1]
        cap = min(tok_dev, 8 * ((3 * tok_dev * top_k + 16 * groups - 1) // (16 * groups)))
        n_rows = groups * cap
        kept = (dev_slot >= 0) & (exp_slot >= 0)
        dest = jnp.where(kept, expert_ids * cap + dev_slot, -1)
        hit = jnp.arange(n_rows)[:, None, None] == dest[None, :, :]
        pick = jnp.any(hit, axis=2).astype(jnp.bfloat16)
        gate_bf = gate_wts.astype(jnp.bfloat16).astype(jnp.float32)
        row_gate = jnp.sum(jnp.where(hit, gate_bf[None], 0.0), axis=(1, 2))
        send = jnp.dot(pick, tokens, preferred_element_type=jnp.float32).astype(jnp.bfloat16)
        recv = lax.all_to_all(send.reshape(groups, cap, d_model), "expert", 0, 0, tiled=True)
        x = recv.reshape(n_rows, d_model)
        hid_gate = jnp.dot(x, w_gate[0], preferred_element_type=jnp.float32)
        hid_up = jnp.dot(x, w_up[0], preferred_element_type=jnp.float32)
        hidden = (jax.nn.silu(hid_gate) * hid_up).astype(jnp.bfloat16)
        y = jnp.dot(hidden, w_down[0], preferred_element_type=jnp.float32).astype(jnp.bfloat16)
        back = lax.all_to_all(y.reshape(groups, cap, d_model), "expert", 0, 0, tiled=True)
        z = (back.reshape(n_rows, d_model).astype(jnp.float32) * row_gate[:, None]).astype(jnp.bfloat16)
        out = jnp.einsum("rt,rd->td", pick, z, preferred_element_type=jnp.float32)
        return out.astype(jnp.bfloat16)

    def moe_layer(*args):
        return jax.shard_map(device_layer, mesh=mesh, in_specs=(row_spec,) * 5 + (weight_spec,) * 3, out_specs=row_spec, check_vma=False)(*args)

    return moe_layer
```

time: 342 us -> 302 us (0.88)
  the two profiles are of different devices: /device:TPU:1 before, /device:TPU:12 now
where the time goes in v1:
time: 302 us; the launch traced here: 301 us
  blocking collectives  118 us (39%)
  waiting for transfers between devices  101 us (33%)
  matrix products  39.1 us (13%)
  other arithmetic  23.5 us (8%)
  starting transfers between devices  16.2 us (5%)
  local copies, waits for them, and re-layouts  3.22 us (1%)
    all_to_all x1, blocking collectives, device_layer(): lax.all_to_all(send.reshape(groups, cap, d_model), 'expert', 0, 0, tiled=...  118 us
    all_to_all x1, waiting for transfers between devices, device_layer(): lax.all_to_all(y.reshape(groups, cap, d_model), 'expert', 0, 0, tiled=True)  101 us
    dot_general x1, matrix products, device_layer(): jnp.dot(hidden, w_down[0], preferred_element_type=jnp.float32)  21.3 us
    all_to_all x1, starting transfers between devices, device_layer(): lax.all_to_all(y.reshape(groups, cap, d_model), 'expert', 0, 0, tiled=True)  16.2 us
    reduce_sum x1, other arithmetic, device_layer(): row_gate = jnp.sum(jnp.where(hit, gate_bf[None], 0.0), axis=(1, 2))  15.2 us
    dot_general x1, matrix products, device_layer(): hid_gate = jnp.dot(x, w_gate[0], preferred_element_type=jnp.float32)  8.55 us
    reduce_or x1, other arithmetic, device_layer(): pick = jnp.any(hit, axis=2).astype(jnp.bfloat16)  7.41 us
  transfers between devices with their start and end apart: 1, of which 1 were waited for; matrix products, arithmetic and copies ran while one was open for 5% of the time, Pallas kernels for 0%

profile of v1, /device:TPU:12, one launch (start us, length us, event | category | flops | bytes accessed | tf_op | source)
XLA Modules:
  0.0 301.4 jit_solution(6136262438501582656)
XLA Ops:
  0.0 0.0 copy-start
  0.0 0.9 add_select_fusion
  0.9 7.4 %fusion.4 = pred[2048,128]{1,0:T(8,128)(4,1)S(1)} fusion(s32[128,8]{0,1:T(8,128)S(1)} %add_select_fusion), kind=kLoop, calls=%fused_computation.6 | loop fusion | flops 3932160 | bytes 266240 | tf_op jit(solution)/shard_map/reduce_or | solution.py:20
  8.3 3.4 %convolution_convert_fusion.1 = bf16[2048,2048]{1,0:T(8,128)(2,1)S(1)} fusion(pred[2048,128]{1,0:T(8,128)(4,1)S(1)} %fusion.4, bf16[128,2048]{1,0:T(8,128)(2,1)} %param.8), kind=kOutput, calls=%fused_computation.8 | convolution fusion | flops 1077936128 | bytes 9175040 | tf_op jit(solution)/shard_map/dot_general | solution.py:23
  11.7 0.0 copy-start.3
  11.7 118.2 %all_to_all.10 = bf16[128,16,2048]{2,1,0:T(8,128)(2,1)S(1)} all-to-all(bf16[128,16,2048]{2,1,0:T(8,128)(2,1)S(1)} %bitcast.20), channel_id=1, replica_groups=mesh['data'=1,'expert'=128] {'expert'}, dimensions={0} | all-to-all | bytes 16777216 | tf_op jit(solution)/shard_map/all_to_all | solution.py:24
  129.9 0.0 copy-start.1
  129.9 3.2 %copy-done.1 = bf16[128,16,2048]{2,1,0:T(8,128)(2,1)} copy-done((bf16[128,16,2048]{2,1,0:T(8,128)(2,1)}, bf16[128,16,2048]{2,1,0:T(8,128)(2,1)S(1)}, u32[]{:S(2)}) %copy-start.1) | copy-done | bytes 8388632
  133.1 0.0 copy-done.3
  133.1 8.6 %fusion.8 = f32[2048,768]{1,0:T(8,128)} fusion(bf16[2048,2048]{1,0:T(8,128)(2,1)S(1)} %bitcast.22, bf16[1,2048,768]{2,1,0:T(8,128)(2,1)S(1)} %copy-done.3), kind=kOutput, calls=%fused_computation.12 | convolution fusion | flops 6442450944 | bytes 17825792 | tf_op jit(solution)/shard_map/dot_general | solution.py:26
  141.7 0.0 copy-done
  141.7 21.3 %convolution_convert_fusion = bf16[2048,2048]{1,0:T(8,128)(2,1)} fusion(f32[2048,768]{1,0:T(8,128)} %fusion.8, bf16[2048,2048]{1,0:T(8,128)(2,1)} %bitcast.23, bf16[1,768,2048]{2,1,0:T(8,128)(2,1)S(1)} %copy-done, bf16[1,2048,768]{2,1,0:T(8,128)(2,1)} %param.14), kind=kOutput, calls=%fused_computation.7 | convolution fusion | flops 12898533376 | bytes 29360128 | tf_op jit(solution)/shard_map/dot_general | solution.py:29
  163.0 0.0 copy-start.2
  163.0 16.2 %all-to-all-start.1 = ((bf16[128,16,2048]{2,1,0:T(8,128)(2,1)}), bf16[128,16,2048]{2,1,0:T(8,128)(2,1)}, u32[]{:S(2)}, u32[]{:S(2)}) async-start(bf16[128,16,2048]{2,1,0:T(8,128)(2,1)} %bitcast.21), calls=%async_computation.1 | async-start | bytes 16777216 | tf_op jit(solution)/shard_map/all_to_all | solution.py:30
  179.2 0.0 copy-done.2
  179.2 15.2 %select_reduce_fusion = f32[2048]{0:T(1024)S(1)} fusion(f32[128,8]{0,1:T(8,128)S(1)} %convert_convert_fusion, s32[128,8]{0,1:T(8,128)S(1)} %add_select_fusion), kind=kLoop, calls=%fused_computation.4 | loop fusion | flops 6289408 | bytes 16384 | tf_op jit(solution)/shard_map/reduce_sum | solution.py:22
  194.4 101.1 %all-to-all-done.1 = bf16[128,16,2048]{2,1,0:T(8,128)(2,1)} async-done(((bf16[128,16,2048]{2,1,0:T(8,128)(2,1)}), bf16[128,16,2048]{2,1,0:T(8,128)(2,1)}, u32[]{:S(2)}, u32[]{:S(2)}) %all-to-all-start.1) | async-done | bytes 8388640 | tf_op jit(solution)/shard_map/all_to_all | solution.py:30
  295.5 5.9 %fusion.11 = bf16[128,2048]{1,0:T(8,128)(2,1)} fusion(pred[2048,128]{1,0:T(8,128)(4,1)S(1)} %fusion.4, bf16[2048,2048]{1,0:T(8,128)(2,1)} %bitcast.7, f32[2048]{0:T(1024)S(1)} %select_reduce_fusion), kind=kOutput, calls=%fused_computation.15 | convolution fusion | flops 1086586880 | bytes 9183232 | tf_op jit(solution)/shard_map/rt,rd->td/dot_general | solution.py:32
  (1 shorter events, 0.0 us)
Async XLA Ops:
  0.0 141.7 %copy-start = (bf16[1,768,2048]{2,1,0:T(8,128)(2,1)S(1)}, bf16[1,768,2048]{2,1,0:T(8,128)(2,1)}, u32[]{:S(2)}) copy-start(bf16[1,768,2048]{2,1,0:T(8,128)(2,1)} %param.15) | copy-start | bytes 9437188
  11.7 121.5 %copy-start.3 = (bf16[1,2048,768]{2,1,0:T(8,128)(2,1)S(1)}, bf16[1,2048,768]{2,1,0:T(8,128)(2,1)}, u32[]{:S(2)}) copy-start(bf16[1,2048,768]{2,1,0:T(8,128)(2,1)} %param.13) | copy-start | bytes 9437188
  129.9 3.2 %copy-start.1 = (bf16[128,16,2048]{2,1,0:T(8,128)(2,1)}, bf16[128,16,2048]{2,1,0:T(8,128)(2,1)S(1)}, u32[]{:S(2)}) copy-start(bf16[128,16,2048]{2,1,0:T(8,128)(2,1)S(1)} %all_to_all.10) | copy-start | bytes 25165828
  163.0 16.2 %copy-start.2 = (f32[128,8]{0,1:T(8,128)S(1)}, f32[128,8]{0,1:T(8,128)}, u32[]{:S(2)}) copy-start(f32[128,8]{0,1:T(8,128)} %param.10) | copy-start | bytes 12292
  163.0 132.6 %all-to-all-start.1 = ((bf16[128,16,2048]{2,1,0:T(8,128)(2,1)}), bf16[128,16,2048]{2,1,0:T(8,128)(2,1)}, u32[]{:S(2)}, u32[]{:S(2)}) async-start(bf16[128,16,2048]{2,1,0:T(8,128)(2,1)} %bitcast.21), calls=%async_computation.1 | async-start | bytes 16777216 | tf_op jit(solution)/shard_map/all_to_all | solution.py:30

commit v2 on v1

v2 whole, which is shorter than its diff:
```python
import jax
import jax.numpy as jnp
from jax import lax
from jax.experimental import pallas as pl
from jax.experimental.pallas import tpu as pltpu
from jax.sharding import PartitionSpec as P

STRIDE = (32, 8, 2)
RING = 4
SLOTS = 16
VMEM_CAP = 67043328
BF16 = jnp.bfloat16
F32 = jnp.float32


def rem4(v):
    return lax.rem(v, RING)


class Place:
    def __init__(self):
        self.me = lax.axis_index("expert")
        self.core = lax.rem(self.me, 2)
        self.k = [rem4(lax.div(self.me, s)) for s in STRIDE]

    def peer(self, axis, delta, core=None):
        there = rem4(self.k[axis] + delta + RING)
        dev = self.me + (there - self.k[axis]) * STRIDE[axis]
        return dev if core is None else dev + core - self.core

    def partner(self):
        return self.me + 1 - 2 * self.core

    def barrier(self):
        sem = pltpu.get_barrier_semaphore()
        peers = [self.peer(ax, dl, c) for ax in range(3) for dl in (1, -1) for c in (0, 1)] + [self.partner()]
        for dev in peers:
            pl.semaphore_signal(sem, inc=1, device_id={"expert": dev}, device_id_type=pl.DeviceIdType.MESH)
        pl.semaphore_wait(sem, len(peers))


def remote(src, dst, send, recv, dev):
    return pltpu.make_async_remote_copy(
        src_ref=src, dst_ref=dst, send_sem=send, recv_sem=recv, device_id={"expert": dev}, device_id_type=pl.DeviceIdType.MESH
    )


class Exchange:
    def __init__(self, pc, c, src, land, transit, send, recv, base):
        self.pc, self.c, self.src, self.land, self.transit = pc, c, src, land, transit
        self.send, self.recv, self.base = send, recv, base

    def sems(self, j, s, r):
        at = self.base + j * 9
        return self.send.at[at + s], self.recv.at[at + r]

    def first(self, j):
        pc, c = self.pc, self.c
        kc, h = pc.k[c], pc.core
        mine = self.land.at[j * 8 + kc * 2 + h]
        out = []
        far = rem4(kc + 2)
        for d, dl in enumerate((1, -1)):
            s, r = self.sems(j, 5 + d, 5 + d)
            out.append(remote(self.src.at[j * 8 + far * 2 + d], self.transit.at[d, j], s, r, pc.peer(c, dl)))
        for d, dl in enumerate((1, -1)):
            near = rem4(kc + dl + RING)
            for core in range(2):
                s, r = self.sems(j, 1 + d * 2 + core, 1 + d * 2 + h)
                out.append(remote(self.src.at[j * 8 + near * 2 + core], mine, s, r, pc.peer(c, dl, core)))
        s, r = self.sems(j, 0, 0)
        out.append(remote(self.src.at[j * 8 + kc * 2 + 1 - h], mine, s, r, pc.partner()))
        return out

    def onward(self, j):
        pc, c = self.pc, self.c
        out = []
        for d, dl in enumerate((1, -1)):
            origin = rem4(pc.k[c] - dl + RING)
            s, r = self.sems(j, 7 + d, 7 + pc.core)
            out.append(remote(self.transit.at[d, j], self.land.at[j * 8 + origin * 2 + pc.core], s, r, pc.peer(c, dl, d)))
        return out

    def wait_transit(self, j):
        for d, dl in enumerate((1, -1)):
            s, r = self.sems(j, 5 + d, 5 + d)
            remote(self.transit.at[d, j], self.transit.at[d, j], s, r, self.pc.peer(self.c, dl)).wait_recv()

    def wait_land(self, j):
        pc, c = self.pc, self.c
        kc, h = pc.k[c], pc.core
        other = pc.partner()

        def arrived(n, origin, core):
            s, r = self.sems(j, 0, n)
            block = self.land.at[j * 8 + origin * 2 + core]
            remote(block, block, s, r, other).wait_recv()

        arrived(0, kc, 1 - h)
        for d, dl in enumerate((1, -1)):
            for core in range(2):
                arrived(1 + d * 2 + core, rem4(kc - dl + RING), core)
        for core in range(2):
            arrived(7 + core, rem4(kc + 2), core)

    def wait_sent(self, j):
        for cp in self.first(j) + self.onward(j):
            cp.wait_send()


def slots_of(rows, ids):
    return [ids[n:n + 1, :] == rows for n in range(ids.shape[0])]


def expert_kernel(dims, tok, meta, wg, wu, wd, y0, y1, y2, ma, t0, t1, t2, mm, s0, s1, s2, l0, l1, l2, r0, r1, r2, x, hid,
                  o0, o1, o2, vg, vu, vd, send, recv, here):
    widths, starts = dims
    pc = Place()
    ys, ts, ss, ls, rs, os = (y0, y1, y2), (t0, t1, t2), (s0, s1, s2), (l0, l1, l2), (r0, r1, r2), (o0, o1, o2)
    axes = [(p, (p + 1) % 3, (p + 2) % 3) for p in range(3)]
    k = pc.k
    half = tok.shape[0] // 2
    top_k = meta.shape[0] // 2
    sent = []

    loads = []
    for p, (a, b, c) in enumerate(axes):
        loads.append(pltpu.make_async_copy(tok.at[:, pl.ds(starts[p], widths[p])], ts[p].at[k[b], k[a]], here.at[p]))
        loads.append(pltpu.make_async_copy(meta, mm.at[p, k[b], k[a]], here.at[3 + p]))
    weights = [pltpu.make_async_copy(src.at[0], dst, here.at[6 + n]) for n, (src, dst) in enumerate(((wg, vg), (wu, vu), (wd, vd)))]
    for cp in loads:
        cp.start()
    pc.barrier()
    for cp in loads:
        cp.wait()
    for cp in weights:
        cp.start()

    def push(p, n, ref, dev):
        cp = remote(ref, ref, send.at[p, n], recv.at[p, n], dev)
        cp.start()
        sent.append(cp)

    def got(p, n, ref):
        remote(ref, ref, send.at[p, n], recv.at[p, n], pc.partner()).wait_recv()

    def blk(p, da, db):
        a, b, c = axes[p]
        return ts[p].at[rem4(k[b] + db), rem4(k[a] + da)]

    def part_of(ref, d):
        return ref.at[pl.ds(d * half, half)]

    def up(p, ax):
        return pc.peer(axes[p][ax], 1)

    def down(p, ax):
        return pc.peer(axes[p][ax], -1)

    def along_b(p, da):
        push(p, 7 + da * 3, blk(p, da, 0), up(p, 1))
        push(p, 8 + da * 3, blk(p, da, 0), down(p, 1))

    def meta_of(p, da):
        a, b, c = axes[p]
        return mm.at[p, k[b], rem4(k[a] + da)]

    def meta_row(p, db):
        return mm.at[p, rem4(k[axes[p][1]] + db)]

    for p in range(3):
        push(p, 4, meta_of(p, 0), up(p, 0))
        push(p, 5, meta_of(p, 0), down(p, 0))
        push(p, 0, blk(p, 0, 0), up(p, 0))
        push(p, 1, blk(p, 0, 0), down(p, 0))
    for p in range(3):
        along_b(p, 0)
    for p in range(3):
        got(p, 4, meta_of(p, 3))
        push(p, 6, meta_of(p, 3), up(p, 0))
        got(p, 5, meta_of(p, 1))
    for p in range(3):
        got(p, 0, blk(p, 3, 0))
        push(p, 2, part_of(blk(p, 3, 0), 0), up(p, 0))
        got(p, 1, blk(p, 1, 0))
        push(p, 3, part_of(blk(p, 1, 0), 1), down(p, 0))
    for p in range(3):
        got(p, 6, meta_of(p, 2))
        push(p, 19, meta_row(p, 0), up(p, 1))
        push(p, 20, meta_row(p, 0), down(p, 1))
        along_b(p, 3)
        along_b(p, 1)
    for p in range(3):
        got(p, 7, blk(p, 0, 3))
        push(p, 9, blk(p, 0, 3), up(p, 1))
    for p in range(3):
        got(p, 2, part_of(blk(p, 2, 0), 0))
        got(p, 3, part_of(blk(p, 2, 0), 1))
        along_b(p, 2)
    keep = [pltpu.make_async_copy(mm.at[p, k[axes[p][1]]], ma.at[p], here.at[9 + p]) for p in range(3)]
    for cp in keep:
        cp.start()
    for p in range(3):
        got(p, 19, meta_row(p, 3))
        push(p, 21, meta_row(p, 3), up(p, 1))
    for da in (3, 1):
        for p in range(3):
            got(p, 8 + da * 3, blk(p, da, 1))
            push(p, 9 + da * 3, blk(p, da, 1), down(p, 1))
    for p in range(3):
        got(p, 7 + 6, blk(p, 2, 3))
        push(p, 9 + 6, blk(p, 2, 3), up(p, 1))
    for p in range(3):
        got(p, 20, meta_row(p, 1))
        got(p, 21, meta_row(p, 2))
        got(p, 8, blk(p, 0, 1))
        got(p, 8 + 6, blk(p, 2, 1))
        for da in (3, 1):
            got(p, 7 + da * 3, blk(p, da, 3))
        for da in (0, 3, 1, 2):
            got(p, 9 + da * 3, blk(p, da, 2))

    lines = [Exchange(pc, axes[p][2], ss[p], ls[p], rs[p], send.at[p], recv.at[p], 22) for p in range(3)]
    row = lax.broadcasted_iota(jnp.int32, (8 * SLOTS, tok.shape[0]), 0)

    def picks(j):
        for p, (a, b, c) in enumerate(axes):
            first = SLOTS * (pc.me - k[c] * STRIDE[c] - pc.core)
            rows = (first + (row >> 5) * (SLOTS * STRIDE[c]) + (row & 31)).astype(F32)

            @pl.loop(0, RING)
            def _(bb):
                aa = rem4(j + 2 * RING - k[c] - bb)
                ids = mm[p, bb, aa][:top_k]
                hot = sum(jnp.where(hit, 1.0, 0.0) for hit in slots_of(rows, ids)).astype(BF16)
                got_rows = jnp.dot(hot, ts[p][bb, aa], preferred_element_type=F32).astype(BF16)
                ss[p][pl.ds(j * 8, 8), bb] = got_rows.reshape(8, SLOTS, widths[p])

            own = j * 8 + k[c] * 2 + pc.core
            ls[p][own] = ss[p][own]

    def places(j, zy, core):
        z, yy = lax.div(zy, RING), rem4(zy)
        xx = rem4(j + 2 * RING - z - yy)
        return [(j * 8 + cc * 2 + core, bb) for cc, bb in ((xx, yy), (z, xx), (yy, z))]

    def ffn(j):
        @pl.loop(0, RING * RING)
        def _(zy):
            for core in range(2):
                for p, (cc, bb) in enumerate(places(j, zy, core)):
                    x[pl.ds(pl.multiple_of((zy * 2 + core) * SLOTS, SLOTS), SLOTS), pl.ds(starts[p], widths[p])] = ls[p][cc, bb]

        @pl.loop(0, hid.shape[1] // 256)
        def _(n):
            cols = pl.ds(pl.multiple_of(n * 256, 256), 256)
            g = jnp.dot(x[...], vg[:, cols], preferred_element_type=F32)
            u = jnp.dot(x[...], vu[:, cols], preferred_element_type=F32)
            hid[:, cols] = (g * jax.nn.sigmoid(g) * u).astype(BF16)

        @pl.loop(0, x.shape[1] // 256)
        def _(n):
            cols = pl.ds(pl.multiple_of(n * 256, 256), 256)
            x[:, cols] = jnp.dot(hid[...], vd[:, cols], preferred_element_type=F32).astype(BF16)

        @pl.loop(0, RING * RING)
        def _(zy):
            for core in range(2):
                for p, (cc, bb) in enumerate(places(j, zy, core)):
                    os[p][cc, bb] = x[pl.ds(pl.multiple_of((zy * 2 + core) * SLOTS, SLOTS), SLOTS), pl.ds(starts[p], widths[p])]

    def stores(j):
        return [pltpu.make_async_copy(os[p].at[pl.ds(j * 8, 8)], ys[p].at[pl.ds(j * 8, 8)], here.at[12 + p * RING + j]) for p in range(3)]

    for cp in weights:
        cp.wait()

    @pl.loop(0, RING + 2)
    def _(i):
        @pl.when(i < RING)
        def _():
            picks(i)
            for line in lines:
                for cp in line.first(i):
                    cp.start()

        @pl.when((i >= 1) & (i < RING + 1))
        def _():
            for line in lines:
                line.wait_transit(i - 1)
                for cp in line.onward(i - 1):
                    cp.start()

        @pl.when(i >= 2)
        def _():
            for line in lines:
                line.wait_land(i - 2)
            ffn(i - 2)
            for cp in stores(i - 2):
                cp.start()

    for cp in keep:
        cp.wait()
    for cp in sent:
        cp.wait_send()

    @pl.loop(0, RING)
    def _(j):
        for line in lines:
            line.wait_sent(j)
        for cp in stores(j):
            cp.wait()


def return_kernel(dims, y0, y1, y2, ma, out, l0, l1, l2, r0, r1, r2, m0, m1, m2, b0, b1, b2, a0, a1, a2, f0, f1, f2, g0, g1, g2,
                  z0, z1, z2, hot, send, recv, here):
    widths, starts = dims
    pc = Place()
    ys, ls, rs, ms, bs, sums = (y0, y1, y2), (l0, l1, l2), (r0, r1, r2), (m0, m1, m2), (b0, b1, b2), (a0, a1, a2)
    fars, nears, zs = (f0, f1, f2), (g0, g1, g2), (z0, z1, z2)
    axes = [(p, (p + 1) % 3, (p + 2) % 3) for p in range(3)]
    k = pc.k
    toks = out.shape[0]
    half = toks // 2
    top_k = ma.shape[2] // 2
    lines = [Exchange(pc, axes[p][2], ys[p], ls[p], rs[p], send.at[p], recv.at[p], 0) for p in range(3)]

    def own(p, j):
        at = j * 8 + k[axes[p][2]] * 2 + pc.core
        return pltpu.make_async_copy(ys[p].at[at], ls[p].at[at], here.at[p, j])

    def sems(p, j, n):
        at = 36 + j * 6 + n
        return send.at[p, at], recv.at[p, at]

    def second(p, j):
        b = axes[p][1]
        cps = []
        for d, dl in enumerate((1, -1)):
            far = ls[p].at[pl.ds(j * 8 + d * 4, 4), rem4(k[b] + 2)]
            cps.append(remote(far, bs[p].at[d, j], *sems(p, j, 2 + d), pc.peer(b, dl)))
        for d, dl in enumerate((1, -1)):
            near = ls[p].at[pl.ds(j * 8, 8), rem4(k[b] + dl + RING)]
            cps.append(remote(near, ms[p].at[j * RING + k[b]], *sems(p, j, d), pc.peer(b, dl)))
        return cps

    def far_rows(p, j, d, origin):
        return ms[p].at[j * RING + origin, pl.ds(d * 4, 4)]

    def second_on(p, j):
        b = axes[p][1]
        return [
            remote(bs[p].at[d, j], far_rows(p, j, d, rem4(k[b] - dl + RING)), *sems(p, j, 4 + d), pc.peer(b, dl))
            for d, dl in enumerate((1, -1))
        ]

    def got(ref, pair):
        remote(ref, ref, *pair, pc.partner()).wait_recv()

    row = lax.broadcasted_iota(jnp.int32, (8 * SLOTS, toks), 0)

    def combine(p, j):
        a, b, c = axes[p]
        src = rem4(j + 2 * RING - k[c] - k[b])
        first = SLOTS * (pc.me - k[b] * STRIDE[b] - k[c] * STRIDE[c] - pc.core)
        info = ma[p, src]
        rows = first + (row >> 5) * (SLOTS * STRIDE[c]) + (row & 31)

        @pl.loop(0, RING)
        def _(bb):
            hits = slots_of((rows + bb * (SLOTS * STRIDE[b])).astype(F32), info[:top_k])
            pick = sum(jnp.where(hit, 1.0, 0.0) for hit in hits)
            gate = sum(jnp.where(hit, info[top_k + n:top_k + n + 1, :], 0.0) for n, hit in enumerate(hits))
            gate = jnp.sum(gate, axis=1, keepdims=True)
            at = pl.ds(pl.multiple_of(bb * 8 * SLOTS, 8 * SLOTS), 8 * SLOTS)
            hot[p, at] = pick.astype(BF16)
            zs[p][at] = (ms[p][j * RING + bb].reshape(8 * SLOTS, widths[p]).astype(F32) * gate).astype(BF16)

        sums[p][src] = lax.dot_general(hot[p], zs[p][...], (((0,), (0,)), ((), ())), preferred_element_type=F32)

    pc.barrier()

    @pl.loop(0, 2 * RING)
    def _(i):
        @pl.when(i < RING)
        def _():
            for p in range(3):
                own(p, i).start()
                for cp in lines[p].first(i):
                    cp.start()

        @pl.when((i >= 1) & (i < RING + 1))
        def _():
            for p in range(3):
                lines[p].wait_transit(i - 1)
                for cp in lines[p].onward(i - 1):
                    cp.start()

        @pl.when((i >= 2) & (i < RING + 2))
        def _():
            j = i - 2
            for p in range(3):
                own(p, j).wait()
                lines[p].wait_land(j)
                for cp in second(p, j):
                    cp.start()
                b = axes[p][1]
                ms[p][j * RING + k[b]] = ls[p][pl.ds(j * 8, 8), k[b]]

        @pl.when((i >= 3) & (i < RING + 3))
        def _():
            j = i - 3
            for p in range(3):
                for d in range(2):
                    got(bs[p].at[d, j], sems(p, j, 2 + d))
                for cp in second_on(p, j):
                    cp.start()

        @pl.when(i >= RING)
        def _():
            j = i - RING
            for p in range(3):
                b = axes[p][1]
                for d, dl in enumerate((1, -1)):
                    got(ms[p].at[j * RING + rem4(k[b] - dl + RING)], sems(p, j, d))
                    got(far_rows(p, j, d, rem4(k[b] + 2)), sems(p, j, 4 + d))
                combine(p, j)

    def at_sem(p, n):
        return send.at[p, 60 + n], recv.at[p, 60 + n]

    tail = []
    for p in range(3):
        a = axes[p][0]
        for d, dl in enumerate((1, -1)):
            piece = sums[p].at[rem4(k[a] + 2), pl.ds(d * half, half)]
            cp = remote(piece, fars[p].at[d], *at_sem(p, d), pc.peer(a, dl))
            cp.start()
            tail.append(cp)
    for p in range(3):
        a = axes[p][0]
        for d, dl in enumerate((1, -1)):
            got(fars[p].at[d], at_sem(p, d))
            near = rem4(k[a] + dl + RING)
            rows = pl.ds(d * half, half)
            sums[p][near, rows] = sums[p][near, rows] + fars[p][d]
            cp = remote(sums[p].at[near], nears[p].at[d], *at_sem(p, 2 + d), pc.peer(a, dl))
            cp.start()
            tail.append(cp)
    for p in range(3):
        a = axes[p][0]
        for d in range(2):
            got(nears[p].at[d], at_sem(p, 2 + d))
        out[:, pl.ds(starts[p], widths[p])] = (sums[p][k[a]] + nears[p][0] + nears[p][1]).astype(out.dtype)
    for cp in tail:
        cp.wait_send()

    @pl.loop(0, RING)
    def _(j):
        for p in range(3):
            lines[p].wait_sent(j)
            for cp in second(p, j) + second_on(p, j):
                cp.wait_send()


def solution(mesh):
    row_spec = P(("data", "expert"), None)
    weight_spec = P("expert", None, None)
    any_spec = pl.BlockSpec(memory_space=pl.ANY)
    vmem_spec = pl.BlockSpec(memory_space=pltpu.VMEM)

    def device_layer(tokens, expert_ids, gate_wts, dev_slot, exp_slot, w_gate, w_up, w_down):
        toks, top_k = expert_ids.shape
        d_model, d_ff = w_gate.shape[1:]
        tiles = d_model // 128
        widths = [128 * (tiles - 2 * (tiles // 3)), 128 * (tiles // 3), 128 * (tiles // 3)]
        starts = [0, widths[0], widths[0] + widths[1]]
        dims = (widths, starts)
        kept = (dev_slot >= 0) & (exp_slot >= 0)
        dest = jnp.where(kept, expert_ids * SLOTS + dev_slot, -1).astype(F32)
        gate_bf = lax.reduce_precision(gate_wts, 8, 7)
        meta = jnp.concatenate([dest.T, gate_bf.T], axis=0)
        n_blocks = 2 * RING * RING

        def bufs(*lead, dtype=BF16):
            return [pltpu.VMEM((*lead, w), dtype) for w in widths]

        blocks = [jax.ShapeDtypeStruct((n_blocks, RING, SLOTS, w), BF16) for w in widths]
        *ys, ma = pl.pallas_call(
            lambda *refs: expert_kernel(dims, *refs),
            out_shape=(*blocks, jax.ShapeDtypeStruct((3, RING, 2 * top_k, toks), F32)),
            in_specs=[any_spec] * 5,
            out_specs=(any_spec,) * 4,
            scratch_shapes=[
                *bufs(RING, RING, toks),
                pltpu.VMEM((3, RING, RING, 2 * top_k, toks), F32),
                *bufs(n_blocks, RING, SLOTS),
                *bufs(n_blocks, RING, SLOTS),
                *bufs(2, RING, RING, SLOTS),
                pltpu.VMEM((n_blocks * SLOTS, d_model), BF16),
                pltpu.VMEM((n_blocks * SLOTS, d_ff), BF16),
                *bufs(n_blocks, RING, SLOTS),
                pltpu.VMEM((d_model, d_ff), BF16),
                pltpu.VMEM((d_model, d_ff), BF16),
                pltpu.VMEM((d_ff, d_model), BF16),
                pltpu.SemaphoreType.DMA((3, 58)),
                pltpu.SemaphoreType.DMA((3, 58)),
                pltpu.SemaphoreType.DMA((24,)),
            ],
            compiler_params=pltpu.CompilerParams(collective_id=0, has_side_effects=True, vmem_limit_bytes=VMEM_CAP),
            name="dispatch_ffn",
        )(tokens, meta, w_gate, w_up, w_down)
        return pl.pallas_call(
            lambda *refs: return_kernel(dims, *refs),
            out_shape=jax.ShapeDtypeStruct((toks, d_model), BF16),
            in_specs=[any_spec] * 3 + [vmem_spec],
            out_specs=vmem_spec,
            scratch_shapes=[
                *bufs(n_blocks, RING, SLOTS),
                *bufs(2, RING, RING, SLOTS),
                *bufs(RING * RING, 8, SLOTS),
                *bufs(2, RING, RING, SLOTS),
                *bufs(RING, toks, dtype=F32),
                *bufs(2, toks // 2, dtype=F32),
                *bufs(2, toks, dtype=F32),
                *bufs(n_blocks * SLOTS),
                pltpu.VMEM((3, n_blocks * SLOTS, toks), BF16),
                pltpu.SemaphoreType.DMA((3, 64)),
                pltpu.SemaphoreType.DMA((3, 64)),
                pltpu.SemaphoreType.DMA((3, 4)),
            ],
            compiler_params=pltpu.CompilerParams(collective_id=1, has_side_effects=True, vmem_limit_bytes=VMEM_CAP),
            name="combine_return",
        )(*ys, ma)

    def moe_layer(*args):
        return jax.shard_map(device_layer, mesh=mesh, in_specs=(row_spec,) * 5 + (weight_spec,) * 3, out_specs=row_spec, check_vma=False)(*args)

    return moe_layer
```

time: 302 us -> 198 us (0.66)
  the two profiles are of different devices: /device:TPU:12 before, /device:TPU:1 now
where the time goes in v2:
time: 198 us; the launch traced here: 197 us
  Pallas kernels  193 us (97%)
  other arithmetic  2.02 us (1%)
    pallas_call x1, Pallas kernels, device_layer(): pl.pallas_call(lambda *refs: expert_kernel(dims, *refs), out_shape=(*bloc...  104 us
    pallas_call x1, Pallas kernels, device_layer(): pl.pallas_call(lambda *refs: return_kernel(dims, *refs), out_shape=jax.Sh...  88.9 us

profile of v2, /device:TPU:1, one launch (start us, length us, event | category | flops | bytes accessed | tf_op | source)
XLA Modules:
  0.0 196.5 jit_solution(3522789455261758021)
XLA Ops:
  0.0 0.7 convert_bitcast_fusion
  0.7 0.7 reduce-precision_bitcast_fusion
  1.4 0.6 pad_maximum_fusion.refs_1_
  2.0 103.7 %dispatch_ffn.1 = (bf16[32,4,16,768]{3,2,1,0:T(8,128)(2,1)}, bf16[32,4,16,640]{3,2,1,0:T(8,128)(2,1)}, bf16[32,4,16,640]{3,2,1,0:T(8,128)(2,1)}, f32[3,4,16,128]{3,2,1,0:T(8,128)}) custom-call(bf16[128,2048]{1,0:T(8,128)(2,1)} %refs_0_.1, f32[16,128]{1,0:T(8,128)} %pad_maximum_fusion.refs_1_, bf16[1,2048,768]{2,1,0:T(8,128)(2,1)} %refs_2_.1, ...), custom_call_target="tpu_custom_call" | custom-call | tf_op jit(solution)/shard_map/dispatch_ffn/pallas_call | solution.py:489
  105.7 88.9 %combine_return.1 = bf16[128,2048]{1,0:T(8,128)(2,1)} custom-call(bf16[32,4,16,768]{3,2,1,0:T(8,128)(2,1)} %get-tuple-element.9.refs_0_, bf16[32,4,16,640]{3,2,1,0:T(8,128)(2,1)} %get-tuple-element.10.refs_1_, bf16[32,4,16,640]{3,2,1,0:T(8,128)(2,1)} %get-tuple-element.11.refs_2_, f32[3,4,16,128]{3,2,1,0:T(8,128)} %get-tuple-element.12.refs_3_), custom_call_target="tpu_custom_call" | custom-call | tf_op jit(solution)/shard_map/combine_return/pallas_call | solution.py:513
  194.6 1.9 copy.10

commit v3 on v1

v3 whole, which is shorter than its diff:
```python
import jax
import jax.numpy as jnp
from jax import lax
from jax.experimental import pallas as pl
from jax.experimental.pallas import tpu as pltpu
from jax.sharding import PartitionSpec as P

STRIDE = (32, 8, 2)
RING = 4
SLOTS = 16
STEPS = (2, 1, -1)
VMEM_CAP = 67043328
BF16 = jnp.bfloat16
F32 = jnp.float32


def rem4(v):
    return lax.rem(v, RING)


class Place:
    def __init__(self):
        self.me = lax.axis_index("expert")
        self.core = lax.rem(self.me, 2)
        self.k = [rem4(lax.div(self.me, s)) for s in STRIDE]

    def peer(self, axis, delta, core=None):
        there = rem4(self.k[axis] + delta + RING)
        dev = self.me + (there - self.k[axis]) * STRIDE[axis]
        return dev if core is None else dev + core - self.core

    def partner(self):
        return self.me + 1 - 2 * self.core

    def barrier(self):
        sem = pltpu.get_barrier_semaphore()
        peers = [self.peer(ax, dl, c) for ax in range(3) for dl in STEPS for c in (0, 1)] + [self.partner()]
        for dev in peers:
            pl.semaphore_signal(sem, inc=1, device_id={"expert": dev}, device_id_type=pl.DeviceIdType.MESH)
        pl.semaphore_wait(sem, len(peers))


def remote(src, dst, send, recv, dev):
    return pltpu.make_async_remote_copy(
        src_ref=src, dst_ref=dst, send_sem=send, recv_sem=recv, device_id={"expert": dev}, device_id_type=pl.DeviceIdType.MESH
    )


class Exchange:
    def __init__(self, pc, c, block, land, send, recv, base):
        self.pc, self.c, self.block, self.land = pc, c, block, land
        self.send, self.recv, self.base = send, recv, base

    def own(self, j):
        return j * 8 + self.pc.k[self.c] * 2 + self.pc.core

    def sends(self, j):
        pc, c = self.pc, self.c
        at = self.base + j * 7
        mine = self.land.at[self.own(j)]
        out = []
        for n, dl in enumerate(STEPS):
            there = rem4(pc.k[c] + dl + RING)
            for core in range(2):
                sems = self.send.at[at + n * 2 + core], self.recv.at[at + n * 2 + pc.core]
                out.append(remote(self.block(j * 8 + there * 2 + core), mine, *sems, pc.peer(c, dl, core)))
        sems = self.send.at[at + 6], self.recv.at[at + 6]
        out.append(remote(self.block(j * 8 + pc.k[c] * 2 + 1 - pc.core), mine, *sems, pc.partner()))
        return out

    def wait_land(self, j):
        pc, c = self.pc, self.c
        at = self.base + j * 7

        def arrived(n, origin, core):
            block = self.land.at[j * 8 + origin * 2 + core]
            remote(block, block, self.send.at[at], self.recv.at[at + n], pc.partner()).wait_recv()

        arrived(6, pc.k[c], 1 - pc.core)
        for n, dl in enumerate(STEPS):
            for core in range(2):
                arrived(n * 2 + core, rem4(pc.k[c] - dl + RING), core)


def slots_of(rows, ids):
    return [ids[n:n + 1, :] == rows for n in range(ids.shape[0])]


SEM_B = 10
SEM_C = 22
SEM_R = SEM_C + 28
SEM_S = SEM_R + 28
SEM_A = SEM_S + 12
N_SEMS = SEM_A + 6


def layer_kernel(dims, tok, meta, wg, wu, wd, out, t0, t1, t2, mm, s0, s1, s2, l0, l1, l2, x, hid, vg, vu, vd, c0, c1, c2,
                 m0, m1, m2, a0, a1, a2, f0, f1, f2, g0, g1, g2, hot, send, recv, here):
    widths, starts = dims
    pc = Place()
    ts, ss, ls, cs, ms, sums = (t0, t1, t2), (s0, s1, s2), (l0, l1, l2), (c0, c1, c2), (m0, m1, m2), (a0, a1, a2)
    fars, nears = (f0, f1, f2), (g0, g1, g2)
    axes = [(p, (p + 1) % 3, (p + 2) % 3) for p in range(3)]
    k = pc.k
    toks = mm.shape[-1]
    top_k = meta.shape[0] // 2
    half = toks // 2
    sent = []

    def spot(p, da, db):
        a, b, c = axes[p]
        return rem4(k[b] + db) * RING + rem4(k[a] + da)

    def blk(p, da, db):
        return ts[p].at[pl.ds(spot(p, da, db) * 8, 8)]

    def half_blk(p, da, db, d):
        return ts[p].at[pl.ds(spot(p, da, db) * 8 + d * 4, 4)]

    loads = []
    for p, (a, b, c) in enumerate(axes):
        loads.append(pltpu.make_async_copy(tok.at[:, :, pl.ds(starts[p], widths[p])], blk(p, 0, 0), here.at[p]))
        loads.append(pltpu.make_async_copy(meta, mm.at[p, k[b], k[a]], here.at[3 + p]))
    weights = [pltpu.make_async_copy(src.at[0], dst, here.at[6 + n]) for n, (src, dst) in enumerate(((wg, vg), (wu, vu), (wd, vd)))]
    for cp in loads:
        cp.start()
    with jax.named_scope("barrier"):
        pc.barrier()
    for cp in loads:
        cp.wait()

    def push(p, n, ref, dev):
        cp = remote(ref, ref, send.at[p, n], recv.at[p, n], dev)
        cp.start()
        sent.append(cp)

    def got(p, n, ref):
        remote(ref, ref, send.at[p, n], recv.at[p, n], pc.partner()).wait_recv()

    def meta_of(p, da):
        return mm.at[p, k[axes[p][1]], rem4(k[axes[p][0]] + da + RING)]

    def meta_row(p, db):
        return mm.at[p, rem4(k[axes[p][1]] + db + RING)]

    def b_sem(da, n):
        return SEM_B + da * 3 + n

    def along_b(p, da):
        push(p, b_sem(da, 0), blk(p, da, 0), pc.peer(axes[p][1], 1))
        push(p, b_sem(da, 1), blk(p, da, 0), pc.peer(axes[p][1], -1))

    def b_low(p, da):
        got(p, b_sem(da, 0), blk(p, da, 3))
        if da in (0, 2):
            push(p, b_sem(da, 2), blk(p, da, 3), pc.peer(axes[p][1], 1))

    def b_high(p, da):
        got(p, b_sem(da, 1), blk(p, da, 1))
        if da in (1, 3):
            push(p, b_sem(da, 2), blk(p, da, 1), pc.peer(axes[p][1], -1))

    def b_far(p, da):
        got(p, b_sem(da, 2), blk(p, da, 2))

    row = lax.broadcasted_iota(jnp.int32, (8 * SLOTS, toks), 0)

    def pick(p, da, db):
        a, b, c = axes[p]
        aa, bb = rem4(k[a] + da), rem4(k[b] + db)
        j = rem4(aa + bb + k[c])
        first = SLOTS * (pc.me - k[c] * STRIDE[c] - pc.core)
        rows = (first + (row >> 5) * (SLOTS * STRIDE[c]) + (row & 31)).astype(F32)
        ids = mm[p, bb, aa][:top_k]
        chosen = sum(jnp.where(hit, 1.0, 0.0) for hit in slots_of(rows, ids)).astype(BF16)
        block = ts[p][pl.ds((bb * RING + aa) * 8, 8)].reshape(toks, widths[p])
        picked = jnp.dot(chosen, block, preferred_element_type=F32).astype(BF16)
        ss[p][pl.ds(j * 8, 8), bb] = picked.reshape(8, SLOTS, widths[p])

    def sides(p, da):
        @pl.loop(0, 2)
        def _(q):
            pick(p, da, 3 - 2 * q)

    for p in range(3):
        for n, dl in enumerate(STEPS):
            push(p, n, meta_of(p, 0), pc.peer(axes[p][0], dl))
        push(p, 6, blk(p, 0, 0), pc.peer(axes[p][0], 1))
        push(p, 7, blk(p, 0, 0), pc.peer(axes[p][0], -1))
    for p in range(3):
        along_b(p, 0)
    for cp in weights:
        cp.start()
    with jax.named_scope("ag_a"):
        for p in range(3):
            got(p, 6, blk(p, 3, 0))
            along_b(p, 3)
            push(p, 8, half_blk(p, 3, 0, 0), pc.peer(axes[p][0], 1))
            got(p, 7, blk(p, 1, 0))
            along_b(p, 1)
            push(p, 9, half_blk(p, 1, 0, 1), pc.peer(axes[p][0], -1))
    with jax.named_scope("ag_meta"):
        for p in range(3):
            for n, dl in enumerate(STEPS):
                got(p, n, meta_of(p, -dl))
            for n, dl in enumerate(STEPS):
                push(p, 3 + n, meta_row(p, 0), pc.peer(axes[p][1], dl))
    with jax.named_scope("ag_b0"):
        for p in range(3):
            b_low(p, 0)
            b_high(p, 0)
    with jax.named_scope("ag_a2"):
        for p in range(3):
            got(p, 8, half_blk(p, 2, 0, 0))
            got(p, 9, half_blk(p, 2, 0, 1))
            along_b(p, 2)
    with jax.named_scope("pick0"):
        for p in range(3):
            @pl.loop(0, RING)
            def _(q):
                pick(p, q, 0)
    for p in range(3):
        for n, dl in enumerate(STEPS):
            got(p, 3 + n, meta_row(p, -dl))
    for da in (3, 1):
        with jax.named_scope("ag_b13"):
            for p in range(3):
                b_low(p, da)
                b_high(p, da)
        with jax.named_scope("pick13"):
            for p in range(3):
                sides(p, 0 if da == 3 else 3)
    with jax.named_scope("ag_b2"):
        for p in range(3):
            b_far(p, 0)
            b_low(p, 2)
    with jax.named_scope("pick2"):
        for p in range(3):
            sides(p, 1)
            pick(p, 0, 2)
    with jax.named_scope("ag_b3"):
        for p in range(3):
            b_high(p, 2)
            b_far(p, 3)
            b_far(p, 1)
    with jax.named_scope("pick3"):
        for p in range(3):
            sides(p, 2)

            @pl.loop(0, 2)
            def _(q):
                pick(p, 1 + 2 * q, 2)
    with jax.named_scope("ag_b4"):
        for p in range(3):
            b_far(p, 2)
            pick(p, 2, 2)

    to_expert = [
        Exchange(pc, axes[p][2], (lambda n, p=p: ss[p].at[n]), ls[p], send.at[p], recv.at[p], SEM_C) for p in range(3)
    ]
    to_source = [
        Exchange(pc, axes[p][2], (lambda n, p=p: ts[p].at[pl.ds(n * RING, RING)]), cs[p], send.at[p], recv.at[p], SEM_R)
        for p in range(3)
    ]

    with jax.named_scope("issue"):
        @pl.loop(0, RING)
        def _(j):
            for p, line in enumerate(to_expert):
                for cp in line.sends(j):
                    cp.start()
                ls[p][line.own(j)] = ss[p][line.own(j)]

    for cp in weights:
        cp.wait()
    for cp in sent:
        cp.wait_send()

    def places(j, zy, core):
        z, yy = lax.div(zy, RING), rem4(zy)
        xx = rem4(j + 2 * RING - z - yy)
        return [(j * 8 + cc * 2 + core, bb) for cc, bb in ((xx, yy), (z, xx), (yy, z))]

    def ffn(j):
        @pl.loop(0, RING * RING)
        def _(zy):
            for core in range(2):
                for p, (at, bb) in enumerate(places(j, zy, core)):
                    x[pl.ds(pl.multiple_of((zy * 2 + core) * SLOTS, SLOTS), SLOTS), pl.ds(starts[p], widths[p])] = ls[p][at, bb]

        @pl.loop(0, hid.shape[1] // 256)
        def _(n):
            cols = pl.ds(pl.multiple_of(n * 256, 256), 256)
            g = jnp.dot(x[...], vg[:, cols], preferred_element_type=F32)
            u = jnp.dot(x[...], vu[:, cols], preferred_element_type=F32)
            hid[:, cols] = (g * jax.nn.sigmoid(g) * u).astype(BF16)

        @pl.loop(0, x.shape[1] // 256)
        def _(n):
            cols = pl.ds(pl.multiple_of(n * 256, 256), 256)
            x[:, cols] = jnp.dot(hid[...], vd[:, cols], preferred_element_type=F32).astype(BF16)

        @pl.loop(0, RING * RING)
        def _(zy):
            for core in range(2):
                for p, (at, bb) in enumerate(places(j, zy, core)):
                    ts[p][at * RING + bb] = x[pl.ds(pl.multiple_of((zy * 2 + core) * SLOTS, SLOTS), SLOTS), pl.ds(starts[p], widths[p])]

    @pl.loop(0, RING)
    def _(j):
        with jax.named_scope("land"):
            for line in to_expert:
                line.wait_land(j)
        with jax.named_scope("ffn"):
            ffn(j)
        with jax.named_scope("send2"):
            for p, line in enumerate(to_source):
                for cp in line.sends(j):
                    cp.start()
                cs[p][line.own(j)] = ts[p][pl.ds(line.own(j) * RING, RING)]

    def second(p, j):
        b = axes[p][1]
        return [
            remote(cs[p].at[pl.ds(j * 8, 8), rem4(k[b] + dl + RING)], ms[p].at[j * RING + k[b]],
                   send.at[p, SEM_S + j * 3 + n], recv.at[p, SEM_S + j * 3 + n], pc.peer(b, dl))
            for n, dl in enumerate(STEPS)
        ]

    @pl.loop(0, RING)
    def _(j):
        with jax.named_scope("land2"):
            for p, line in enumerate(to_source):
                line.wait_land(j)
                for cp in second(p, j):
                    cp.start()
        for p in range(3):
            kb = k[axes[p][1]]
            ms[p][j * RING + kb] = cs[p][pl.ds(j * 8, 8), kb]

    def combine(p, j):
        a, b, c = axes[p]
        src = rem4(j + 2 * RING - k[c] - k[b])
        first = SLOTS * (pc.me - k[b] * STRIDE[b] - k[c] * STRIDE[c] - pc.core)
        info = mm[p, k[b], src]
        rows = first + (row >> 5) * (SLOTS * STRIDE[c]) + (row & 31)
        cols = pl.ds(starts[p], widths[p])

        @pl.loop(0, RING)
        def _(bb):
            hits = slots_of((rows + bb * (SLOTS * STRIDE[b])).astype(F32), info[:top_k])
            chosen = sum(jnp.where(hit, 1.0, 0.0) for hit in hits)
            gate = sum(jnp.where(hit, info[top_k + n:top_k + n + 1, :], 0.0) for n, hit in enumerate(hits))
            gate = jnp.sum(gate, axis=1, keepdims=True)
            at = pl.ds(pl.multiple_of(bb * 8 * SLOTS, 8 * SLOTS), 8 * SLOTS)
            hot[p, at] = chosen.astype(BF16)
            x[at, cols] = (ms[p][j * RING + bb].reshape(8 * SLOTS, widths[p]).astype(F32) * gate).astype(BF16)

        sums[p][src] = lax.dot_general(hot[p], x[:, cols], (((0,), (0,)), ((), ())), preferred_element_type=F32)

    @pl.loop(0, RING)
    def _(j):
        for p in range(3):
            with jax.named_scope("arrive"):
                for n, dl in enumerate(STEPS):
                    got(p, SEM_S + j * 3 + n, ms[p].at[j * RING + rem4(k[axes[p][1]] - dl + RING)])
            with jax.named_scope("combine"):
                combine(p, j)

    tail = []

    def hand(p, n, ref, dst, dl):
        cp = remote(ref, dst, send.at[p, SEM_A + n], recv.at[p, SEM_A + n], pc.peer(axes[p][0], dl))
        cp.start()
        tail.append(cp)

    sides_of = ((0, 1), (1, -1))
    for p in range(3):
        ka = k[axes[p][0]]
        for d, dl in sides_of:
            hand(p, d, sums[p].at[rem4(ka + 2), pl.ds(d * half, half)], fars[p].at[d], dl)
        for d, dl in sides_of:
            rows = pl.ds((1 - d) * half, half)
            hand(p, 2 + d, sums[p].at[rem4(ka + dl + RING), rows], nears[p].at[d, rows], dl)
    with jax.named_scope("rs1"):
        for p in range(3):
            ka = k[axes[p][0]]
            for d, dl in sides_of:
                got(p, SEM_A + d, fars[p].at[d])
                near = rem4(ka + dl + RING)
                rows = pl.ds(d * half, half)
                sums[p][near, rows] = sums[p][near, rows] + fars[p][d]
                hand(p, 4 + d, sums[p].at[near, rows], nears[p].at[d, rows], dl)
    with jax.named_scope("rs2"):
        for p in range(3):
            for d, dl in sides_of:
                got(p, SEM_A + 2 + d, nears[p].at[d, pl.ds((1 - d) * half, half)])
                got(p, SEM_A + 4 + d, nears[p].at[d, pl.ds(d * half, half)])
            out[:, pl.ds(starts[p], widths[p])] = (sums[p][k[axes[p][0]]] + nears[p][0] + nears[p][1]).astype(out.dtype)
    with jax.named_scope("drain"):
        for cp in tail:
            cp.wait_send()

        @pl.loop(0, RING)
        def _(j):
            for p in range(3):
                for cp in to_expert[p].sends(j) + to_source[p].sends(j) + second(p, j):
                    cp.wait_send()


def solution(mesh):
    row_spec = P(("data", "expert"), None)
    weight_spec = P("expert", None, None)
    any_spec = pl.BlockSpec(memory_space=pl.ANY)

    def device_layer(tokens, expert_ids, gate_wts, dev_slot, exp_slot, w_gate, w_up, w_down):
        toks, top_k = expert_ids.shape
        d_model, d_ff = w_gate.shape[1:]
        tiles = d_model // 128
        widths = [128 * (tiles - 2 * (tiles // 3)), 128 * (tiles // 3), 128 * (tiles // 3)]
        starts = [0, widths[0], widths[0] + widths[1]]
        dims = (widths, starts)
        kept = (dev_slot >= 0) & (exp_slot >= 0)
        dest = jnp.where(kept, expert_ids * SLOTS + dev_slot, -1).astype(F32)
        gate_bf = lax.reduce_precision(gate_wts, 8, 7)
        meta = jnp.concatenate([dest.T, gate_bf.T], axis=0)
        n_blocks = 2 * RING * RING

        def bufs(*lead, dtype=BF16):
            return [pltpu.VMEM((*lead, w), dtype) for w in widths]

        return pl.pallas_call(
            lambda *refs: layer_kernel(dims, *refs),
            out_shape=jax.ShapeDtypeStruct((toks, d_model), BF16),
            in_specs=[any_spec] * 5,
            out_specs=pl.BlockSpec(memory_space=pltpu.VMEM),
            scratch_shapes=[
                *bufs(n_blocks * RING, SLOTS),
                pltpu.VMEM((3, RING, RING, 2 * top_k, toks), F32),
                *bufs(n_blocks, RING, SLOTS),
                *bufs(n_blocks, RING, SLOTS),
                pltpu.VMEM((n_blocks * SLOTS, d_model), BF16),
                pltpu.VMEM((n_blocks * SLOTS, d_ff), BF16),
                pltpu.VMEM((d_model, d_ff), BF16),
                pltpu.VMEM((d_model, d_ff), BF16),
                pltpu.VMEM((d_ff, d_model), BF16),
                *bufs(n_blocks, RING, SLOTS),
                *bufs(RING * RING, 8, SLOTS),
                *bufs(RING, toks, dtype=F32),
                *bufs(2, toks // 2, dtype=F32),
                *bufs(2, toks, dtype=F32),
                pltpu.VMEM((3, n_blocks * SLOTS, toks), BF16),
                pltpu.SemaphoreType.DMA((3, N_SEMS)),
                pltpu.SemaphoreType.DMA((3, N_SEMS)),
                pltpu.SemaphoreType.DMA((9,)),
            ],
            compiler_params=pltpu.CompilerParams(collective_id=0, has_side_effects=True, vmem_limit_bytes=VMEM_CAP),
            name="moe_layer",
        )(tokens.reshape(toks // SLOTS, SLOTS, d_model), meta, w_gate, w_up, w_down)

    def moe_layer(*args):
        return jax.shard_map(device_layer, mesh=mesh, in_specs=(row_spec,) * 5 + (weight_spec,) * 3, out_specs=row_spec, check_vma=False)(*args)

    return moe_layer
```

time: 302 us -> 169 us (0.56)
  the two profiles are of different devices: /device:TPU:12 before, /device:TPU:1 now
where the time goes in v3:
time: 169 us
  Pallas kernels  165 us (98%)
  other arithmetic  2.02 us (1%)
  local copies, waits for them, and re-layouts  1.88 us (1%)
    pallas_call x1, Pallas kernels, device_layer(): pl.pallas_call(lambda *refs: layer_kernel(dims, *refs), out_shape=jax.Sha...  165 us

profile of v3, /device:TPU:1, one launch (start us, length us, event | category | flops | bytes accessed | tf_op | source)
XLA Modules:
  0.0 168.6 jit_solution(2727604627475363406)
XLA Ops:
  0.0 0.7 convert_bitcast_fusion
  0.7 0.7 reduce-precision_bitcast_fusion
  1.4 0.6 pad_maximum_fusion.refs_1_
  2.0 164.7 %moe_layer.1 = bf16[128,2048]{1,0:T(8,128)(2,1)} custom-call(bf16[8,16,2048]{2,1,0:T(8,128)(2,1)} %bitcast.5, f32[16,128]{1,0:T(8,128)} %pad_maximum_fusion.refs_1_, bf16[1,2048,768]{2,1,0:T(8,128)(2,1)} %refs_2_.1, bf16[1,2048,768]{2,1,0:T(8,128)(2,1)} %refs_3_.1, bf16[1,768,2048]{2,1,0:T(8,128)(2,1)} %refs_4_.1), custom_call_target="tpu_custom_call" | custom-call | tf_op jit(solution)/shard_map/moe_layer/pallas_call | solution.py:432
  166.7 1.9 %copy.10 = bf16[128,2048]{1,0:T(8,128)(2,1)} copy(bf16[128,2048]{1,0:T(8,128)(2,1)} %moe_layer.1) | data formatting | bytes 1048576

commit v4 on v3

--- a/solution.py
+++ b/solution.py
@@ -32,12 +32,15 @@
     def partner(self):
         return self.me + 1 - 2 * self.core
 
-    def barrier(self):
+    def greet(self):
         sem = pltpu.get_barrier_semaphore()
         peers = [self.peer(ax, dl, c) for ax in range(3) for dl in STEPS for c in (0, 1)] + [self.partner()]
+        self.n_peers = len(peers)
         for dev in peers:
             pl.semaphore_signal(sem, inc=1, device_id={"expert": dev}, device_id_type=pl.DeviceIdType.MESH)
-        pl.semaphore_wait(sem, len(peers))
+
+    def meet(self):
+        pl.semaphore_wait(pltpu.get_barrier_semaphore(), self.n_peers)
 
 
 def remote(src, dst, send, recv, dev):
@@ -94,16 +97,17 @@
 N_SEMS = SEM_A + 6
 
 
-def layer_kernel(dims, tok, meta, wg, wu, wd, out, t0, t1, t2, mm, s0, s1, s2, l0, l1, l2, x, hid, vg, vu, vd, c0, c1, c2,
-                 m0, m1, m2, a0, a1, a2, f0, f1, f2, g0, g1, g2, hot, send, recv, here):
+def layer_kernel(dims, tok, ids, devs, exps, gates, wg, wu, wd, out, t0, t1, t2, mm, s0, s1, s2, l0, l1, l2, x, hid, vg, vu, vd, c0, c1, c2,
+                 m0, m1, m2, a0, a1, a2, f0, f1, f2, g0, g1, g2, hot, raw, hot_gate, send, recv, here):
     widths, starts = dims
     pc = Place()
     ts, ss, ls, cs, ms, sums = (t0, t1, t2), (s0, s1, s2), (l0, l1, l2), (c0, c1, c2), (m0, m1, m2), (a0, a1, a2)
     fars, nears = (f0, f1, f2), (g0, g1, g2)
     axes = [(p, (p + 1) % 3, (p + 2) % 3) for p in range(3)]
+    back = [axes[(p + 2) % 3] for p in range(3)]
     k = pc.k
     toks = mm.shape[-1]
-    top_k = meta.shape[0] // 2
+    top_k = ids.shape[0]
     half = toks // 2
     sent = []
 
@@ -117,17 +121,27 @@
     def half_blk(p, da, db, d):
         return ts[p].at[pl.ds(spot(p, da, db) * 8 + d * 4, 4)]
 
-    loads = []
-    for p, (a, b, c) in enumerate(axes):
-        loads.append(pltpu.make_async_copy(tok.at[:, :, pl.ds(starts[p], widths[p])], blk(p, 0, 0), here.at[p]))
-        loads.append(pltpu.make_async_copy(meta, mm.at[p, k[b], k[a]], here.at[3 + p]))
-    weights = [pltpu.make_async_copy(src.at[0], dst, here.at[6 + n]) for n, (src, dst) in enumerate(((wg, vg), (wu, vu), (wd, vd)))]
-    for cp in loads:
+    loads = [
+        pltpu.make_async_copy(tok.at[:, :, pl.ds(starts[p], widths[p])], blk(p, 0, 0), here.at[p]) for p in range(3)
+    ]
+    routes = [pltpu.make_async_copy(src, raw.at[n], here.at[6 + n]) for n, src in enumerate((ids, devs, exps))]
+    routes.append(pltpu.make_async_copy(gates, hot_gate, here.at[9]))
+    weights = [pltpu.make_async_copy(src.at[0], dst, here.at[3 + n]) for n, (src, dst) in enumerate(((wg, vg), (wu, vu), (wd, vd)))]
+    for cp in routes + loads:
         cp.start()
     with jax.named_scope("barrier"):
-        pc.barrier()
-    for cp in loads:
-        cp.wait()
+        pc.greet()
+        for cp in routes:
+            cp.wait()
+        kept = (raw[1] >= 0) & (raw[2] >= 0)
+        dest = jnp.where(kept, raw[0] * SLOTS + raw[1], -1).astype(F32)
+        gate_bf = hot_gate[...].astype(BF16).astype(F32)
+        for p, (a, b, c) in enumerate(axes):
+            mm[p, k[b], k[a], pl.ds(0, top_k)] = dest
+            mm[p, k[b], k[a], pl.ds(top_k, top_k)] = gate_bf
+        for cp in loads:
+            cp.wait()
+        pc.meet()
 
     def push(p, n, ref, dev):
         cp = remote(ref, ref, send.at[p, n], recv.at[p, n], dev)
@@ -191,37 +205,43 @@
         along_b(p, 0)
     for cp in weights:
         cp.start()
-    with jax.named_scope("ag_a"):
-        for p in range(3):
-            got(p, 6, blk(p, 3, 0))
-            along_b(p, 3)
-            push(p, 8, half_blk(p, 3, 0, 0), pc.peer(axes[p][0], 1))
-            got(p, 7, blk(p, 1, 0))
-            along_b(p, 1)
-            push(p, 9, half_blk(p, 1, 0, 1), pc.peer(axes[p][0], -1))
     with jax.named_scope("ag_meta"):
         for p in range(3):
             for n, dl in enumerate(STEPS):
                 got(p, n, meta_of(p, -dl))
             for n, dl in enumerate(STEPS):
                 push(p, 3 + n, meta_row(p, 0), pc.peer(axes[p][1], dl))
-    with jax.named_scope("ag_b0"):
-        for p in range(3):
-            b_low(p, 0)
-            b_high(p, 0)
+    with jax.named_scope("ag_a"):
+        for p in range(3):
+            got(p, 6, blk(p, 3, 0))
+            push(p, 8, half_blk(p, 3, 0, 0), pc.peer(axes[p][0], 1))
+            got(p, 7, blk(p, 1, 0))
+            push(p, 9, half_blk(p, 1, 0, 1), pc.peer(axes[p][0], -1))
+        for p in range(3):
+            along_b(p, 3)
+        for p in range(3):
+            along_b(p, 1)
+    with jax.named_scope("pick0"):
+        for p in range(3):
+            @pl.loop(0, 3)
+            def _(q):
+                pick(p, q + lax.div(q, 2), 0)
     with jax.named_scope("ag_a2"):
         for p in range(3):
             got(p, 8, half_blk(p, 2, 0, 0))
             got(p, 9, half_blk(p, 2, 0, 1))
             along_b(p, 2)
-    with jax.named_scope("pick0"):
-        for p in range(3):
-            @pl.loop(0, RING)
-            def _(q):
-                pick(p, q, 0)
+    with jax.named_scope("ag_b0"):
+        for p in range(3):
+            b_low(p, 0)
+            b_high(p, 0)
     for p in range(3):
         for n, dl in enumerate(STEPS):
             got(p, 3 + n, meta_row(p, -dl))
+    with jax.named_scope("pick1"):
+        for p in range(3):
+            pick(p, 2, 0)
+            sides(p, 0)
     for da in (3, 1):
         with jax.named_scope("ag_b13"):
             for p in range(3):
@@ -229,44 +249,44 @@
                 b_high(p, da)
         with jax.named_scope("pick13"):
             for p in range(3):
-                sides(p, 0 if da == 3 else 3)
+                sides(p, da)
     with jax.named_scope("ag_b2"):
         for p in range(3):
-            b_far(p, 0)
             b_low(p, 2)
+            b_high(p, 2)
     with jax.named_scope("pick2"):
         for p in range(3):
-            sides(p, 1)
-            pick(p, 0, 2)
-    with jax.named_scope("ag_b3"):
-        for p in range(3):
-            b_high(p, 2)
-            b_far(p, 3)
-            b_far(p, 1)
-    with jax.named_scope("pick3"):
-        for p in range(3):
             sides(p, 2)
-
-            @pl.loop(0, 2)
-            def _(q):
-                pick(p, 1 + 2 * q, 2)
-    with jax.named_scope("ag_b4"):
-        for p in range(3):
-            b_far(p, 2)
-            pick(p, 2, 2)
-
     to_expert = [
         Exchange(pc, axes[p][2], (lambda n, p=p: ss[p].at[n]), ls[p], send.at[p], recv.at[p], SEM_C) for p in range(3)
     ]
     to_source = [
-        Exchange(pc, axes[p][2], (lambda n, p=p: ts[p].at[pl.ds(n * RING, RING)]), cs[p], send.at[p], recv.at[p], SEM_R)
+        Exchange(pc, back[p][2], (lambda n, p=p: ts[p].at[pl.ds(n * RING, RING)]), cs[p], send.at[p], recv.at[p], SEM_R)
         for p in range(3)
     ]
 
-    with jax.named_scope("issue"):
-        @pl.loop(0, RING)
-        def _(j):
-            for p, line in enumerate(to_expert):
+    with jax.named_scope("ag_b3"):
+        for p in range(3):
+            b_far(p, 0)
+            b_far(p, 3)
+    with jax.named_scope("pick3"):
+        for p in range(3):
+            @pl.loop(0, 2)
+            def _(q):
+                pick(p, 3 * q, 2)
+    for p in (1, 2, 0):
+        with jax.named_scope("ag_b4"):
+            b_far(p, 1)
+            b_far(p, 2)
+        with jax.named_scope("pick4"):
+            @pl.loop(0, 2)
+            def _(q):
+                pick(p, 1 + q, 2)
+
+            line = to_expert[p]
+
+            @pl.loop(0, RING)
+            def _(j):
                 for cp in line.sends(j):
                     cp.start()
                 ls[p][line.own(j)] = ss[p][line.own(j)]
@@ -276,16 +296,16 @@
     for cp in sent:
         cp.wait_send()
 
-    def places(j, zy, core):
+    def places(order, j, zy, core):
         z, yy = lax.div(zy, RING), rem4(zy)
-        xx = rem4(j + 2 * RING - z - yy)
-        return [(j * 8 + cc * 2 + core, bb) for cc, bb in ((xx, yy), (z, xx), (yy, z))]
+        at = (z, yy, rem4(j + 2 * RING - z - yy))
+        return [(j * 8 + at[c] * 2 + core, at[b]) for a, b, c in order]
 
     def ffn(j):
         @pl.loop(0, RING * RING)
         def _(zy):
             for core in range(2):
-                for p, (at, bb) in enumerate(places(j, zy, core)):
+                for p, (at, bb) in enumerate(places(axes, j, zy, core)):
                     x[pl.ds(pl.multiple_of((zy * 2 + core) * SLOTS, SLOTS), SLOTS), pl.ds(starts[p], widths[p])] = ls[p][at, bb]
 
         @pl.loop(0, hid.shape[1] // 256)
@@ -303,7 +323,7 @@
         @pl.loop(0, RING * RING)
         def _(zy):
             for core in range(2):
-                for p, (at, bb) in enumerate(places(j, zy, core)):
+                for p, (at, bb) in enumerate(places(back, j, zy, core)):
                     ts[p][at * RING + bb] = x[pl.ds(pl.multiple_of((zy * 2 + core) * SLOTS, SLOTS), SLOTS), pl.ds(starts[p], widths[p])]
 
     @pl.loop(0, RING)
@@ -320,7 +340,7 @@
                 cs[p][line.own(j)] = ts[p][pl.ds(line.own(j) * RING, RING)]
 
     def second(p, j):
-        b = axes[p][1]
+        b = back[p][1]
         return [
             remote(cs[p].at[pl.ds(j * 8, 8), rem4(k[b] + dl + RING)], ms[p].at[j * RING + k[b]],
                    send.at[p, SEM_S + j * 3 + n], recv.at[p, SEM_S + j * 3 + n], pc.peer(b, dl))
@@ -335,14 +355,14 @@
                 for cp in second(p, j):
                     cp.start()
         for p in range(3):
-            kb = k[axes[p][1]]
+            kb = k[back[p][1]]
             ms[p][j * RING + kb] = cs[p][pl.ds(j * 8, 8), kb]
 
     def combine(p, j):
-        a, b, c = axes[p]
+        a, b, c = back[p]
         src = rem4(j + 2 * RING - k[c] - k[b])
         first = SLOTS * (pc.me - k[b] * STRIDE[b] - k[c] * STRIDE[c] - pc.core)
-        info = mm[p, k[b], src]
+        info = mm[(p + 2) % 3, k[b], src]
         rows = first + (row >> 5) * (SLOTS * STRIDE[c]) + (row & 31)
         cols = pl.ds(starts[p], widths[p])
 
@@ -358,25 +378,29 @@
 
         sums[p][src] = lax.dot_general(hot[p], x[:, cols], (((0,), (0,)), ((), ())), preferred_element_type=F32)
 
-    @pl.loop(0, RING)
+    def gathered(p, j):
+        with jax.named_scope("arrive"):
+            for n, dl in enumerate(STEPS):
+                got(p, SEM_S + j * 3 + n, ms[p].at[j * RING + rem4(k[back[p][1]] - dl + RING)])
+        with jax.named_scope("combine"):
+            combine(p, j)
+
+    @pl.loop(0, RING - 1)
     def _(j):
         for p in range(3):
-            with jax.named_scope("arrive"):
-                for n, dl in enumerate(STEPS):
-                    got(p, SEM_S + j * 3 + n, ms[p].at[j * RING + rem4(k[axes[p][1]] - dl + RING)])
-            with jax.named_scope("combine"):
-                combine(p, j)
+            gathered(p, j)
 
     tail = []
 
     def hand(p, n, ref, dst, dl):
-        cp = remote(ref, dst, send.at[p, SEM_A + n], recv.at[p, SEM_A + n], pc.peer(axes[p][0], dl))
+        cp = remote(ref, dst, send.at[p, SEM_A + n], recv.at[p, SEM_A + n], pc.peer(back[p][0], dl))
         cp.start()
         tail.append(cp)
 
     sides_of = ((0, 1), (1, -1))
     for p in range(3):
-        ka = k[axes[p][0]]
+        gathered(p, RING - 1)
+        ka = k[back[p][0]]
         for d, dl in sides_of:
             hand(p, d, sums[p].at[rem4(ka + 2), pl.ds(d * half, half)], fars[p].at[d], dl)
         for d, dl in sides_of:
@@ -384,7 +408,7 @@
             hand(p, 2 + d, sums[p].at[rem4(ka + dl + RING), rows], nears[p].at[d, rows], dl)
     with jax.named_scope("rs1"):
         for p in range(3):
-            ka = k[axes[p][0]]
+            ka = k[back[p][0]]
             for d, dl in sides_of:
                 got(p, SEM_A + d, fars[p].at[d])
                 near = rem4(ka + dl + RING)
@@ -396,7 +420,7 @@
             for d, dl in sides_of:
                 got(p, SEM_A + 2 + d, nears[p].at[d, pl.ds((1 - d) * half, half)])
                 got(p, SEM_A + 4 + d, nears[p].at[d, pl.ds(d * half, half)])
-            out[:, pl.ds(starts[p], widths[p])] = (sums[p][k[axes[p][0]]] + nears[p][0] + nears[p][1]).astype(out.dtype)
+            out[:, pl.ds(starts[p], widths[p])] = sums[p][k[back[p][0]]] + nears[p][0] + nears[p][1]
     with jax.named_scope("drain"):
         for cp in tail:
             cp.wait_send()
@@ -420,19 +444,15 @@
         widths = [128 * (tiles - 2 * (tiles // 3)), 128 * (tiles // 3), 128 * (tiles // 3)]
         starts = [0, widths[0], widths[0] + widths[1]]
         dims = (widths, starts)
-        kept = (dev_slot >= 0) & (exp_slot >= 0)
-        dest = jnp.where(kept, expert_ids * SLOTS + dev_slot, -1).astype(F32)
-        gate_bf = lax.reduce_precision(gate_wts, 8, 7)
-        meta = jnp.concatenate([dest.T, gate_bf.T], axis=0)
         n_blocks = 2 * RING * RING
 
         def bufs(*lead, dtype=BF16):
             return [pltpu.VMEM((*lead, w), dtype) for w in widths]
 
-        return pl.pallas_call(
+        summed = pl.pallas_call(
             lambda *refs: layer_kernel(dims, *refs),
-            out_shape=jax.ShapeDtypeStruct((toks, d_model), BF16),
-            in_specs=[any_spec] * 5,
+            out_shape=jax.ShapeDtypeStruct((toks, d_model), F32),
+            in_specs=[any_spec] * 8,
             out_specs=pl.BlockSpec(memory_space=pltpu.VMEM),
             scratch_shapes=[
                 *bufs(n_blocks * RING, SLOTS),
@@ -450,13 +470,16 @@
                 *bufs(2, toks // 2, dtype=F32),
                 *bufs(2, toks, dtype=F32),
                 pltpu.VMEM((3, n_blocks * SLOTS, toks), BF16),
+                pltpu.VMEM((3, top_k, toks), jnp.int32),
+                pltpu.VMEM((top_k, toks), F32),
                 pltpu.SemaphoreType.DMA((3, N_SEMS)),
                 pltpu.SemaphoreType.DMA((3, N_SEMS)),
-                pltpu.SemaphoreType.DMA((9,)),
+                pltpu.SemaphoreType.DMA((10,)),
             ],
             compiler_params=pltpu.CompilerParams(collective_id=0, has_side_effects=True, vmem_limit_bytes=VMEM_CAP),
             name="moe_layer",
-        )(tokens.reshape(toks // SLOTS, SLOTS, d_model), meta, w_gate, w_up, w_down)
+        )(tokens.reshape(toks // SLOTS, SLOTS, d_model), expert_ids.T, dev_slot.T, exp_slot.T, gate_wts.T, w_gate, w_up, w_down)
+        return summed.astype(BF16)
 
     def moe_layer(*args):
         return jax.shard_map(device_layer, mesh=mesh, in_specs=(row_spec,) * 5 + (weight_spec,) * 3, out_specs=row_spec, check_vma=False)(*args)

time: 169 us -> 156 us (0.923)
  Pallas kernels: 165 us -> 154 us
  local copies, waits for them, and re-layouts: 1.88 us -> 0 us
    pallas_call x1, Pallas kernels: 165 us -> 154 us  [device_layer(): pl.pallas_call(lambda *refs: layer_kernel(dims, *refs), out_shape=jax.Sha...]
    convert_element_type x0 -> x1, other arithmetic: none -> 2.09 us  [device_layer(): return summed.astype(BF16)]
    unnamed x1 -> x0, local copies, waits for them, and re-layouts: 1.88 us -> none
where the time goes in v4:
time: 156 us
  Pallas kernels  154 us (99%)
  other arithmetic  2.09 us (1%)
    pallas_call x1, Pallas kernels, device_layer(): pl.pallas_call(lambda *refs: layer_kernel(dims, *refs), out_shape=jax.Sha...  154 us

profile of v4, /device:TPU:1, one launch (start us, length us, event | category | flops | bytes accessed | tf_op | source)
XLA Modules:
  0.0 156.2 jit_solution(17391355425522390859)
XLA Ops:
  0.0 154.1 %moe_layer.1 = f32[128,2048]{1,0:T(8,128)} custom-call(bf16[8,16,2048]{2,1,0:T(8,128)(2,1)} %bitcast.5, s32[8,128]{1,0:T(8,128)} %bitcast.6, s32[8,128]{1,0:T(8,128)} %bitcast.7, s32[8,128]{1,0:T(8,128)} %bitcast.8, f32[8,128]{1,0:T(8,128)} %bitcast.9, bf16[1,2048,768]{2,1,0:T(8,128)(2,1)} %refs_5_.1, bf16[1,2048,768]{2,1,0:T(8,128)(2,1)} %refs_6_.1, ...), custom_call_target="tpu_custom_call" | custom-call | tf_op jit(solution)/shard_map/moe_layer/pallas_call | solution.py:452
  154.1 2.1 %convert_element_type.3 = bf16[128,2048]{1,0:T(8,128)(2,1)} convert(f32[128,2048]{1,0:T(8,128)} %moe_layer.1) | non-fusion elementwise | flops 262144 | bytes 1572864 | tf_op jit(solution)/shard_map/convert_element_type | solution.py:482

commit v5 on v4

--- a/solution.py
+++ b/solution.py
@@ -59,46 +59,35 @@
 
     def sends(self, j):
         pc, c = self.pc, self.c
-        at = self.base + j * 7
+        sems = self.send, self.recv.at[self.base + j]
         mine = self.land.at[self.own(j)]
         out = []
-        for n, dl in enumerate(STEPS):
+        for dl in STEPS:
             there = rem4(pc.k[c] + dl + RING)
             for core in range(2):
-                sems = self.send.at[at + n * 2 + core], self.recv.at[at + n * 2 + pc.core]
                 out.append(remote(self.block(j * 8 + there * 2 + core), mine, *sems, pc.peer(c, dl, core)))
-        sems = self.send.at[at + 6], self.recv.at[at + 6]
         out.append(remote(self.block(j * 8 + pc.k[c] * 2 + 1 - pc.core), mine, *sems, pc.partner()))
         return out
 
     def wait_land(self, j):
-        pc, c = self.pc, self.c
-        at = self.base + j * 7
-
-        def arrived(n, origin, core):
-            block = self.land.at[j * 8 + origin * 2 + core]
-            remote(block, block, self.send.at[at], self.recv.at[at + n], pc.partner()).wait_recv()
-
-        arrived(6, pc.k[c], 1 - pc.core)
-        for n, dl in enumerate(STEPS):
-            for core in range(2):
-                arrived(n * 2 + core, rem4(pc.k[c] - dl + RING), core)
+        rows = self.land.at[pl.ds(j * 8, 7)]
+        remote(rows, rows, self.send, self.recv.at[self.base + j], self.pc.partner()).wait_recv()
+
+    def wait_sent(self):
+        rows = self.land.at[pl.ds(0, 7 * RING)]
+        remote(rows, rows, self.send, self.recv.at[self.base], self.pc.partner()).wait_send()
 
 
 def slots_of(rows, ids):
     return [ids[n:n + 1, :] == rows for n in range(ids.shape[0])]
 
 
-SEM_B = 10
-SEM_C = 22
-SEM_R = SEM_C + 28
-SEM_S = SEM_R + 28
-SEM_A = SEM_S + 12
-N_SEMS = SEM_A + 6
+R_META, R_A, R_FAR, R_SIDES, R_ENDS, R_C, R_BACK, R_B, R_SUM, N_RECV = 0, 2, 4, 5, 9, 11, 15, 19, 23, 25
+S_META, S_GATHER, S_C, S_BACK, S_B, S_SUM, N_SEND = 0, 2, 3, 4, 5, 6, 7
 
 
 def layer_kernel(dims, tok, ids, devs, exps, gates, wg, wu, wd, out, t0, t1, t2, mm, s0, s1, s2, l0, l1, l2, x, hid, vg, vu, vd, c0, c1, c2,
-                 m0, m1, m2, a0, a1, a2, f0, f1, f2, g0, g1, g2, hot, raw, hot_gate, send, recv, here):
+                 m0, m1, m2, a0, a1, a2, f0, f1, f2, g0, g1, g2, hot, scale, raw, hot_gate, send, recv, here):
     widths, starts = dims
     pc = Place()
     ts, ss, ls, cs, ms, sums = (t0, t1, t2), (s0, s1, s2), (l0, l1, l2), (c0, c1, c2), (m0, m1, m2), (a0, a1, a2)
@@ -109,7 +98,6 @@
     toks = mm.shape[-1]
     top_k = ids.shape[0]
     half = toks // 2
-    sent = []
 
     def spot(p, da, db):
         a, b, c = axes[p]
@@ -143,40 +131,34 @@
             cp.wait()
         pc.meet()
 
-    def push(p, n, ref, dev):
-        cp = remote(ref, ref, send.at[p, n], recv.at[p, n], dev)
-        cp.start()
-        sent.append(cp)
-
-    def got(p, n, ref):
-        remote(ref, ref, send.at[p, n], recv.at[p, n], pc.partner()).wait_recv()
+    def push(p, s, r, ref, dev):
+        remote(ref, ref, send.at[p, s], recv.at[p, r], dev).start()
+
+    def got(p, r, ref):
+        remote(ref, ref, send.at[p, 0], recv.at[p, r], pc.partner()).wait_recv()
+
+    def gone(p, s, ref):
+        remote(ref, ref, send.at[p, s], recv.at[p, 0], pc.partner()).wait_send()
+
+    def some(p, n):
+        return ts[p].at[pl.ds(0, n * 8)]
 
     def meta_of(p, da):
         return mm.at[p, k[axes[p][1]], rem4(k[axes[p][0]] + da + RING)]
 
-    def meta_row(p, db):
-        return mm.at[p, rem4(k[axes[p][1]] + db + RING)]
-
-    def b_sem(da, n):
-        return SEM_B + da * 3 + n
-
     def along_b(p, da):
-        push(p, b_sem(da, 0), blk(p, da, 0), pc.peer(axes[p][1], 1))
-        push(p, b_sem(da, 1), blk(p, da, 0), pc.peer(axes[p][1], -1))
-
-    def b_low(p, da):
-        got(p, b_sem(da, 0), blk(p, da, 3))
-        if da in (0, 2):
-            push(p, b_sem(da, 2), blk(p, da, 3), pc.peer(axes[p][1], 1))
-
-    def b_high(p, da):
-        got(p, b_sem(da, 1), blk(p, da, 1))
-        if da in (1, 3):
-            push(p, b_sem(da, 2), blk(p, da, 1), pc.peer(axes[p][1], -1))
-
-    def b_far(p, da):
-        got(p, b_sem(da, 2), blk(p, da, 2))
-
+        for dl in (1, -1):
+            push(p, S_GATHER, R_SIDES + da, blk(p, da, 0), pc.peer(axes[p][1], dl))
+
+    def b_sides(p, da):
+        got(p, R_SIDES + da, some(p, 2))
+        dl = 1 if da in (0, 2) else -1
+        push(p, S_GATHER, R_ENDS + (da in (1, 2)), blk(p, da, 3 if dl == 1 else 1), pc.peer(axes[p][1], dl))
+
+    def b_ends(p, n):
+        got(p, R_ENDS + n, some(p, 2))
+
+    early = rem4(k[0] + k[1] + k[2] + 2)
     row = lax.broadcasted_iota(jnp.int32, (8 * SLOTS, toks), 0)
 
     def pick(p, da, db):
@@ -196,27 +178,35 @@
         def _(q):
             pick(p, da, 3 - 2 * q)
 
+    to_expert = [
+        Exchange(pc, axes[p][2], (lambda n, p=p: ss[p].at[n]), ls[p], send.at[p, S_C], recv.at[p], R_C) for p in range(3)
+    ]
+    def offer(p, j):
+        line = to_expert[p]
+        for cp in line.sends(j):
+            cp.start()
+        ls[p][line.own(j)] = ss[p][line.own(j)]
+
     for p in range(3):
-        for n, dl in enumerate(STEPS):
-            push(p, n, meta_of(p, 0), pc.peer(axes[p][0], dl))
-        push(p, 6, blk(p, 0, 0), pc.peer(axes[p][0], 1))
-        push(p, 7, blk(p, 0, 0), pc.peer(axes[p][0], -1))
+        for dl in STEPS:
+            push(p, S_META, R_META, meta_of(p, 0), pc.peer(axes[p][0], dl))
+        push(p, S_GATHER, R_A, blk(p, 0, 0), pc.peer(axes[p][0], 1))
+        push(p, S_GATHER, R_A + 1, blk(p, 0, 0), pc.peer(axes[p][0], -1))
     for p in range(3):
         along_b(p, 0)
     for cp in weights:
         cp.start()
     with jax.named_scope("ag_meta"):
         for p in range(3):
-            for n, dl in enumerate(STEPS):
-                got(p, n, meta_of(p, -dl))
-            for n, dl in enumerate(STEPS):
-                push(p, 3 + n, meta_row(p, 0), pc.peer(axes[p][1], dl))
+            got(p, R_META, mm.at[p, 0, pl.ds(0, 3)])
+            for dl in STEPS:
+                push(p, S_META + 1, R_META + 1, mm.at[p, k[axes[p][1]]], pc.peer(axes[p][1], dl))
     with jax.named_scope("ag_a"):
         for p in range(3):
-            got(p, 6, blk(p, 3, 0))
-            push(p, 8, half_blk(p, 3, 0, 0), pc.peer(axes[p][0], 1))
-            got(p, 7, blk(p, 1, 0))
-            push(p, 9, half_blk(p, 1, 0, 1), pc.peer(axes[p][0], -1))
+            got(p, R_A, blk(p, 3, 0))
+            push(p, S_GATHER, R_FAR, half_blk(p, 3, 0, 0), pc.peer(axes[p][0], 1))
+            got(p, R_A + 1, blk(p, 1, 0))
+            push(p, S_GATHER, R_FAR, half_blk(p, 1, 0, 1), pc.peer(axes[p][0], -1))
         for p in range(3):
             along_b(p, 3)
         for p in range(3):
@@ -228,16 +218,13 @@
                 pick(p, q + lax.div(q, 2), 0)
     with jax.named_scope("ag_a2"):
         for p in range(3):
-            got(p, 8, half_blk(p, 2, 0, 0))
-            got(p, 9, half_blk(p, 2, 0, 1))
+            got(p, R_FAR, blk(p, 2, 0))
             along_b(p, 2)
     with jax.named_scope("ag_b0"):
         for p in range(3):
-            b_low(p, 0)
-            b_high(p, 0)
+            b_sides(p, 0)
     for p in range(3):
-        for n, dl in enumerate(STEPS):
-            got(p, 3 + n, meta_row(p, -dl))
+        got(p, R_META + 1, mm.at[p, pl.ds(0, 3)])
     with jax.named_scope("pick1"):
         for p in range(3):
             pick(p, 2, 0)
@@ -245,56 +232,49 @@
     for da in (3, 1):
         with jax.named_scope("ag_b13"):
             for p in range(3):
-                b_low(p, da)
-                b_high(p, da)
+                b_sides(p, da)
         with jax.named_scope("pick13"):
             for p in range(3):
                 sides(p, da)
     with jax.named_scope("ag_b2"):
         for p in range(3):
-            b_low(p, 2)
-            b_high(p, 2)
+            b_sides(p, 2)
     with jax.named_scope("pick2"):
         for p in range(3):
             sides(p, 2)
-    to_expert = [
-        Exchange(pc, axes[p][2], (lambda n, p=p: ss[p].at[n]), ls[p], send.at[p], recv.at[p], SEM_C) for p in range(3)
-    ]
     to_source = [
-        Exchange(pc, back[p][2], (lambda n, p=p: ts[p].at[pl.ds(n * RING, RING)]), cs[p], send.at[p], recv.at[p], SEM_R)
+        Exchange(pc, back[p][2], (lambda n, p=p: ts[p].at[pl.ds(n * RING, RING)]), cs[p], send.at[p, S_BACK], recv.at[p], R_BACK)
         for p in range(3)
     ]
 
     with jax.named_scope("ag_b3"):
         for p in range(3):
-            b_far(p, 0)
-            b_far(p, 3)
+            b_ends(p, 0)
     with jax.named_scope("pick3"):
         for p in range(3):
             @pl.loop(0, 2)
             def _(q):
                 pick(p, 3 * q, 2)
+
+            offer(p, early)
     for p in (1, 2, 0):
         with jax.named_scope("ag_b4"):
-            b_far(p, 1)
-            b_far(p, 2)
+            b_ends(p, 1)
         with jax.named_scope("pick4"):
             @pl.loop(0, 2)
             def _(q):
                 pick(p, 1 + q, 2)
 
-            line = to_expert[p]
-
-            @pl.loop(0, RING)
-            def _(j):
-                for cp in line.sends(j):
-                    cp.start()
-                ls[p][line.own(j)] = ss[p][line.own(j)]
+            @pl.loop(0, RING - 1)
+            def _(q):
+                offer(p, q + lax.div(q + RING - early, RING))
 
     for cp in weights:
         cp.wait()
-    for cp in sent:
-        cp.wait_send()
+    for p in range(3):
+        gone(p, S_META, mm.at[p, 0, pl.ds(0, 3)])
+        gone(p, S_META + 1, mm.at[p, pl.ds(0, 3)])
+        gone(p, S_GATHER, some(p, 15))
 
     def places(order, j, zy, core):
         z, yy = lax.div(zy, RING), rem4(zy)
@@ -308,17 +288,10 @@
                 for p, (at, bb) in enumerate(places(axes, j, zy, core)):
                     x[pl.ds(pl.multiple_of((zy * 2 + core) * SLOTS, SLOTS), SLOTS), pl.ds(starts[p], widths[p])] = ls[p][at, bb]
 
-        @pl.loop(0, hid.shape[1] // 256)
-        def _(n):
-            cols = pl.ds(pl.multiple_of(n * 256, 256), 256)
-            g = jnp.dot(x[...], vg[:, cols], preferred_element_type=F32)
-            u = jnp.dot(x[...], vu[:, cols], preferred_element_type=F32)
-            hid[:, cols] = (g * jax.nn.sigmoid(g) * u).astype(BF16)
-
-        @pl.loop(0, x.shape[1] // 256)
-        def _(n):
-            cols = pl.ds(pl.multiple_of(n * 256, 256), 256)
-            x[:, cols] = jnp.dot(hid[...], vd[:, cols], preferred_element_type=F32).astype(BF16)
+        g = jnp.dot(x[...], vg[...], preferred_element_type=F32)
+        u = jnp.dot(x[...], vu[...], preferred_element_type=F32)
+        hid[...] = (g * jax.nn.sigmoid(g) * u).astype(BF16)
+        x[...] = jnp.dot(hid[...], vd[...], preferred_element_type=F32).astype(BF16)
 
         @pl.loop(0, RING * RING)
         def _(zy):
@@ -343,8 +316,8 @@
         b = back[p][1]
         return [
             remote(cs[p].at[pl.ds(j * 8, 8), rem4(k[b] + dl + RING)], ms[p].at[j * RING + k[b]],
-                   send.at[p, SEM_S + j * 3 + n], recv.at[p, SEM_S + j * 3 + n], pc.peer(b, dl))
-            for n, dl in enumerate(STEPS)
+                   send.at[p, S_B], recv.at[p, R_B + j], pc.peer(b, dl))
+            for dl in STEPS
         ]
 
     @pl.loop(0, RING)
@@ -358,78 +331,84 @@
             kb = k[back[p][1]]
             ms[p][j * RING + kb] = cs[p][pl.ds(j * 8, 8), kb]
 
-    def combine(p, j):
+    def prepare(p, j):
         a, b, c = back[p]
         src = rem4(j + 2 * RING - k[c] - k[b])
         first = SLOTS * (pc.me - k[b] * STRIDE[b] - k[c] * STRIDE[c] - pc.core)
         info = mm[(p + 2) % 3, k[b], src]
         rows = first + (row >> 5) * (SLOTS * STRIDE[c]) + (row & 31)
-        cols = pl.ds(starts[p], widths[p])
 
         @pl.loop(0, RING)
         def _(bb):
             hits = slots_of((rows + bb * (SLOTS * STRIDE[b])).astype(F32), info[:top_k])
             chosen = sum(jnp.where(hit, 1.0, 0.0) for hit in hits)
             gate = sum(jnp.where(hit, info[top_k + n:top_k + n + 1, :], 0.0) for n, hit in enumerate(hits))
-            gate = jnp.sum(gate, axis=1, keepdims=True)
             at = pl.ds(pl.multiple_of(bb * 8 * SLOTS, 8 * SLOTS), 8 * SLOTS)
             hot[p, at] = chosen.astype(BF16)
-            x[at, cols] = (ms[p][j * RING + bb].reshape(8 * SLOTS, widths[p]).astype(F32) * gate).astype(BF16)
+            scale[p, at] = jnp.sum(gate, axis=1, keepdims=True)
+
+    def combine(p, j):
+        a, b, c = back[p]
+        src = rem4(j + 2 * RING - k[c] - k[b])
+        cols = pl.ds(starts[p], widths[p])
+
+        @pl.loop(0, RING)
+        def _(bb):
+            at = pl.ds(pl.multiple_of(bb * 8 * SLOTS, 8 * SLOTS), 8 * SLOTS)
+            x[at, cols] = (ms[p][j * RING + bb].reshape(8 * SLOTS, widths[p]).astype(F32) * scale[p, at]).astype(BF16)
 
         sums[p][src] = lax.dot_general(hot[p], x[:, cols], (((0,), (0,)), ((), ())), preferred_element_type=F32)
 
     def gathered(p, j):
         with jax.named_scope("arrive"):
-            for n, dl in enumerate(STEPS):
-                got(p, SEM_S + j * 3 + n, ms[p].at[j * RING + rem4(k[back[p][1]] - dl + RING)])
+            got(p, R_B + j, ms[p].at[pl.ds(j * RING, 3)])
         with jax.named_scope("combine"):
             combine(p, j)
 
+    def prepared(j):
+        with jax.named_scope("prepare"):
+            for p in range(3):
+                prepare(p, j)
+
     @pl.loop(0, RING - 1)
     def _(j):
+        prepared(j)
         for p in range(3):
             gathered(p, j)
 
-    tail = []
-
-    def hand(p, n, ref, dst, dl):
-        cp = remote(ref, dst, send.at[p, SEM_A + n], recv.at[p, SEM_A + n], pc.peer(back[p][0], dl))
-        cp.start()
-        tail.append(cp)
+    prepared(RING - 1)
+
+    def hand(p, r, ref, dst, dl):
+        remote(ref, dst, send.at[p, S_SUM], recv.at[p, R_SUM + r], pc.peer(back[p][0], dl)).start()
 
     sides_of = ((0, 1), (1, -1))
     for p in range(3):
         gathered(p, RING - 1)
         ka = k[back[p][0]]
         for d, dl in sides_of:
-            hand(p, d, sums[p].at[rem4(ka + 2), pl.ds(d * half, half)], fars[p].at[d], dl)
+            hand(p, 0, sums[p].at[rem4(ka + 2), pl.ds(d * half, half)], fars[p].at[d], dl)
         for d, dl in sides_of:
             rows = pl.ds((1 - d) * half, half)
-            hand(p, 2 + d, sums[p].at[rem4(ka + dl + RING), rows], nears[p].at[d, rows], dl)
+            hand(p, 1, sums[p].at[rem4(ka + dl + RING), rows], nears[p].at[d, rows], dl)
     with jax.named_scope("rs1"):
         for p in range(3):
             ka = k[back[p][0]]
+            got(p, R_SUM, fars[p])
             for d, dl in sides_of:
-                got(p, SEM_A + d, fars[p].at[d])
                 near = rem4(ka + dl + RING)
                 rows = pl.ds(d * half, half)
                 sums[p][near, rows] = sums[p][near, rows] + fars[p][d]
-                hand(p, 4 + d, sums[p].at[near, rows], nears[p].at[d, rows], dl)
+                hand(p, 1, sums[p].at[near, rows], nears[p].at[d, rows], dl)
     with jax.named_scope("rs2"):
         for p in range(3):
-            for d, dl in sides_of:
-                got(p, SEM_A + 2 + d, nears[p].at[d, pl.ds((1 - d) * half, half)])
-                got(p, SEM_A + 4 + d, nears[p].at[d, pl.ds(d * half, half)])
-            out[:, pl.ds(starts[p], widths[p])] = sums[p][k[back[p][0]]] + nears[p][0] + nears[p][1]
+            got(p, R_SUM + 1, nears[p])
+            out[:, pl.ds(starts[p], widths[p])] = (sums[p][k[back[p][0]]] + nears[p][0] + nears[p][1]).astype(out.dtype)
     with jax.named_scope("drain"):
-        for cp in tail:
-            cp.wait_send()
-
-        @pl.loop(0, RING)
-        def _(j):
-            for p in range(3):
-                for cp in to_expert[p].sends(j) + to_source[p].sends(j) + second(p, j):
-                    cp.wait_send()
+        for p in range(3):
+            to_expert[p].wait_sent()
+            to_source[p].wait_sent()
+            gone(p, S_B, ms[p].at[pl.ds(0, 3 * RING)])
+            gone(p, S_SUM, sums[p].at[pl.ds(0, 3)])
 
 
 def solution(mesh):
@@ -451,7 +430,7 @@
 
         summed = pl.pallas_call(
             lambda *refs: layer_kernel(dims, *refs),
-            out_shape=jax.ShapeDtypeStruct((toks, d_model), F32),
+            out_shape=jax.ShapeDtypeStruct((toks, d_model), BF16),
             in_specs=[any_spec] * 8,
             out_specs=pl.BlockSpec(memory_space=pltpu.VMEM),
             scratch_shapes=[
@@ -470,16 +449,17 @@
                 *bufs(2, toks // 2, dtype=F32),
                 *bufs(2, toks, dtype=F32),
                 pltpu.VMEM((3, n_blocks * SLOTS, toks), BF16),
+                pltpu.VMEM((3, n_blocks * SLOTS, 1), F32),
                 pltpu.VMEM((3, top_k, toks), jnp.int32),
                 pltpu.VMEM((top_k, toks), F32),
-                pltpu.SemaphoreType.DMA((3, N_SEMS)),
-                pltpu.SemaphoreType.DMA((3, N_SEMS)),
+                pltpu.SemaphoreType.DMA((3, N_SEND)),
+                pltpu.SemaphoreType.DMA((3, N_RECV)),
                 pltpu.SemaphoreType.DMA((10,)),
             ],
             compiler_params=pltpu.CompilerParams(collective_id=0, has_side_effects=True, vmem_limit_bytes=VMEM_CAP),
             name="moe_layer",
         )(tokens.reshape(toks // SLOTS, SLOTS, d_model), expert_ids.T, dev_slot.T, exp_slot.T, gate_wts.T, w_gate, w_up, w_down)
-        return summed.astype(BF16)
+        return summed
 
     def moe_layer(*args):
         return jax.shard_map(device_layer, mesh=mesh, in_specs=(row_spec,) * 5 + (weight_spec,) * 3, out_specs=row_spec, check_vma=False)(*args)

time: 156 us -> 150 us (0.962); the launches traced: 156 us -> 149 us
  Pallas kernels: 154 us -> 147 us
  other arithmetic: 2.09 us -> 0 us
  local copies, waits for them, and re-layouts: 0 us -> 1.88 us
    pallas_call x1, Pallas kernels: 154 us -> 147 us  [device_layer(): pl.pallas_call(lambda *refs: layer_kernel(dims, *refs), out_shape=jax.Sha...]
    convert_element_type x1 -> x0, other arithmetic: 2.09 us -> none  [device_layer(): return summed.astype(BF16)]
    unnamed x0 -> x1, local copies, waits for them, and re-layouts: none -> 1.88 us
where the time goes in v5:
time: 150 us; the launch traced here: 149 us
  Pallas kernels  147 us (98%)
  local copies, waits for them, and re-layouts  1.88 us (1%)
    pallas_call x1, Pallas kernels, device_layer(): pl.pallas_call(lambda *refs: layer_kernel(dims, *refs), out_shape=jax.Sha...  147 us

profile of v5, /device:TPU:1, one launch (start us, length us, event | category | flops | bytes accessed | tf_op | source)
XLA Modules:
  0.0 148.6 jit_solution(16348316386818334645)
XLA Ops:
  0.0 146.7 %moe_layer.1 = bf16[128,2048]{1,0:T(8,128)(2,1)} custom-call(bf16[8,16,2048]{2,1,0:T(8,128)(2,1)} %bitcast.5, s32[8,128]{1,0:T(8,128)} %bitcast.6, s32[8,128]{1,0:T(8,128)} %bitcast.7, s32[8,128]{1,0:T(8,128)} %bitcast.8, f32[8,128]{1,0:T(8,128)} %bitcast.9, bf16[1,2048,768]{2,1,0:T(8,128)(2,1)} %refs_5_.1, bf16[1,2048,768]{2,1,0:T(8,128)(2,1)} %refs_6_.1, ...), custom_call_target="tpu_custom_call" | custom-call | tf_op jit(solution)/shard_map/moe_layer/pallas_call | solution.py:431
  146.7 1.9 %copy.10 = bf16[128,2048]{1,0:T(8,128)(2,1)} copy(bf16[128,2048]{1,0:T(8,128)(2,1)} %moe_layer.1) | data formatting | bytes 1048576

commit v6 on v5

--- a/solution.py
+++ b/solution.py
@@ -9,7 +9,7 @@
 RING = 4
 SLOTS = 16
 STEPS = (2, 1, -1)
-VMEM_CAP = 67043328
+VMEM_CAP = 65930000
 BF16 = jnp.bfloat16
 F32 = jnp.float32
 
@@ -57,17 +57,25 @@
     def own(self, j):
         return j * 8 + self.pc.k[self.c] * 2 + self.pc.core
 
+    def far(self, j):
+        return self.to_ring(j, 2)
+
+    def near(self, j):
+        pc = self.pc
+        sems = self.send, self.recv.at[self.base + j]
+        across = remote(self.block(j * 8 + pc.k[self.c] * 2 + 1 - pc.core), self.land.at[self.own(j)], *sems, pc.partner())
+        return self.to_ring(j, 1) + self.to_ring(j, -1) + [across]
+
+    def to_ring(self, j, dl):
+        pc, c = self.pc, self.c
+        there = rem4(pc.k[c] + dl + RING)
+        sems = self.send, self.recv.at[self.base + j]
+        return [
+            remote(self.block(j * 8 + there * 2 + core), self.land.at[self.own(j)], *sems, pc.peer(c, dl, core)) for core in range(2)
+        ]
+
     def sends(self, j):
-        pc, c = self.pc, self.c
-        sems = self.send, self.recv.at[self.base + j]
-        mine = self.land.at[self.own(j)]
-        out = []
-        for dl in STEPS:
-            there = rem4(pc.k[c] + dl + RING)
-            for core in range(2):
-                out.append(remote(self.block(j * 8 + there * 2 + core), mine, *sems, pc.peer(c, dl, core)))
-        out.append(remote(self.block(j * 8 + pc.k[c] * 2 + 1 - pc.core), mine, *sems, pc.partner()))
-        return out
+        return self.far(j) + self.near(j)
 
     def wait_land(self, j):
         rows = self.land.at[pl.ds(j * 8, 7)]
@@ -82,12 +90,13 @@
     return [ids[n:n + 1, :] == rows for n in range(ids.shape[0])]
 
 
-R_META, R_A, R_FAR, R_SIDES, R_ENDS, R_C, R_BACK, R_B, R_SUM, N_RECV = 0, 2, 4, 5, 9, 11, 15, 19, 23, 25
+R_META, R_A, R_FAR, R_SIDES, R_ENDS, R_BACK, R_B, R_SUM, N_RECV = 0, 2, 4, 5, 9, 11, 15, 20, 24
+R_C = 0
 S_META, S_GATHER, S_C, S_BACK, S_B, S_SUM, N_SEND = 0, 2, 3, 4, 5, 6, 7
 
 
 def layer_kernel(dims, tok, ids, devs, exps, gates, wg, wu, wd, out, t0, t1, t2, mm, s0, s1, s2, l0, l1, l2, x, hid, vg, vu, vd, c0, c1, c2,
-                 m0, m1, m2, a0, a1, a2, f0, f1, f2, g0, g1, g2, hot, scale, raw, hot_gate, send, recv, here):
+                 m0, m1, m2, a0, a1, a2, f0, f1, f2, g0, g1, g2, hot, scale, raw, hot_gate, send, recv, shared, here):
     widths, starts = dims
     pc = Place()
     ts, ss, ls, cs, ms, sums = (t0, t1, t2), (s0, s1, s2), (l0, l1, l2), (c0, c1, c2), (m0, m1, m2), (a0, a1, a2)
@@ -179,13 +188,14 @@
             pick(p, da, 3 - 2 * q)
 
     to_expert = [
-        Exchange(pc, axes[p][2], (lambda n, p=p: ss[p].at[n]), ls[p], send.at[p, S_C], recv.at[p], R_C) for p in range(3)
+        Exchange(pc, axes[p][2], (lambda n, p=p: ss[p].at[n]), ls[p], send.at[p, S_C], shared, R_C) for p in range(3)
     ]
-    def offer(p, j):
+    def offer(p, j, far=True, near=True):
         line = to_expert[p]
-        for cp in line.sends(j):
+        for cp in (line.far(j) if far else []) + (line.near(j) if near else []):
             cp.start()
-        ls[p][line.own(j)] = ss[p][line.own(j)]
+        if near:
+            ls[p][line.own(j)] = ss[p][line.own(j)]
 
     for p in range(3):
         for dl in STEPS:
@@ -247,17 +257,16 @@
         for p in range(3)
     ]
 
-    with jax.named_scope("ag_b3"):
-        for p in range(3):
+    for p in (2, 1, 0):
+        with jax.named_scope("ag_b3"):
             b_ends(p, 0)
-    with jax.named_scope("pick3"):
-        for p in range(3):
+        with jax.named_scope("pick3"):
             @pl.loop(0, 2)
             def _(q):
                 pick(p, 3 * q, 2)
 
-            offer(p, early)
-    for p in (1, 2, 0):
+            offer(p, early, near=p > 0)
+    for p in (2, 1, 0):
         with jax.named_scope("ag_b4"):
             b_ends(p, 1)
         with jax.named_scope("pick4"):
@@ -265,9 +274,18 @@
             def _(q):
                 pick(p, 1 + q, 2)
 
-            @pl.loop(0, RING - 1)
-            def _(q):
-                offer(p, q + lax.div(q + RING - early, RING))
+            if p:
+                @pl.loop(0, RING - 1)
+                def _(q):
+                    offer(p, q + lax.div(q + RING - early, RING))
+            else:
+                @pl.loop(0, RING)
+                def _(j):
+                    @pl.when(j != early)
+                    def _():
+                        offer(p, j, near=False)
+
+                    offer(p, j, far=False)
 
     for cp in weights:
         cp.wait()
@@ -302,8 +320,8 @@
     @pl.loop(0, RING)
     def _(j):
         with jax.named_scope("land"):
-            for line in to_expert:
-                line.wait_land(j)
+            full = x.at[pl.ds(0, 7 * RING * SLOTS)]
+            remote(full, full, send.at[0, S_C], shared.at[R_C + j], pc.partner()).wait_recv()
         with jax.named_scope("ffn"):
             ffn(j)
         with jax.named_scope("send2"):
@@ -312,12 +330,15 @@
                     cp.start()
                 cs[p][line.own(j)] = ts[p][pl.ds(line.own(j) * RING, RING)]
 
+    cut = 128 * ((widths[0] // 128 + 1) // 2)
+    piece = [[pl.ds(0, cut), pl.ds(cut, w - cut)] for w in widths]
+
     def second(p, j):
         b = back[p][1]
         return [
-            remote(cs[p].at[pl.ds(j * 8, 8), rem4(k[b] + dl + RING)], ms[p].at[j * RING + k[b]],
-                   send.at[p, S_B], recv.at[p, R_B + j], pc.peer(b, dl))
-            for dl in STEPS
+            remote(cs[p].at[pl.ds(j * 8, 8), rem4(k[b] + dl + RING), :, piece[p][u]], ms[p].at[j * RING + k[b], :, :, piece[p][u]],
+                   send.at[p, S_B], recv.at[p, R_B + j + u * lax.div(j, RING - 1)], pc.peer(b, dl))
+            for u in range(2) for dl in STEPS
         ]
 
     @pl.loop(0, RING)
@@ -345,25 +366,20 @@
             gate = sum(jnp.where(hit, info[top_k + n:top_k + n + 1, :], 0.0) for n, hit in enumerate(hits))
             at = pl.ds(pl.multiple_of(bb * 8 * SLOTS, 8 * SLOTS), 8 * SLOTS)
             hot[p, at] = chosen.astype(BF16)
-            scale[p, at] = jnp.sum(gate, axis=1, keepdims=True)
-
-    def combine(p, j):
+            scale[at, p:p + 1] = jnp.sum(gate, axis=1, keepdims=True)
+
+    def combine(p, j, cols):
         a, b, c = back[p]
         src = rem4(j + 2 * RING - k[c] - k[b])
-        cols = pl.ds(starts[p], widths[p])
+        xcols = pl.ds(starts[p] + cols.start, cols.size)
 
         @pl.loop(0, RING)
         def _(bb):
             at = pl.ds(pl.multiple_of(bb * 8 * SLOTS, 8 * SLOTS), 8 * SLOTS)
-            x[at, cols] = (ms[p][j * RING + bb].reshape(8 * SLOTS, widths[p]).astype(F32) * scale[p, at]).astype(BF16)
-
-        sums[p][src] = lax.dot_general(hot[p], x[:, cols], (((0,), (0,)), ((), ())), preferred_element_type=F32)
-
-    def gathered(p, j):
-        with jax.named_scope("arrive"):
-            got(p, R_B + j, ms[p].at[pl.ds(j * RING, 3)])
-        with jax.named_scope("combine"):
-            combine(p, j)
+            rows = ms[p][j * RING + bb, :, :, cols].reshape(8 * SLOTS, cols.size)
+            x[at, xcols] = (rows.astype(F32) * scale[at, p:p + 1]).astype(BF16)
+
+        sums[p][src, :, cols] = lax.dot_general(hot[p], x[:, xcols], (((0,), (0,)), ((), ())), preferred_element_type=F32)
 
     def prepared(j):
         with jax.named_scope("prepare"):
@@ -374,7 +390,10 @@
     def _(j):
         prepared(j)
         for p in range(3):
-            gathered(p, j)
+            with jax.named_scope("arrive"):
+                got(p, R_B + j, ms[p].at[pl.ds(j * RING, 3)])
+            with jax.named_scope("combine"):
+                combine(p, j, pl.ds(0, widths[p]))
 
     prepared(RING - 1)
 
@@ -382,27 +401,37 @@
         remote(ref, dst, send.at[p, S_SUM], recv.at[p, R_SUM + r], pc.peer(back[p][0], dl)).start()
 
     sides_of = ((0, 1), (1, -1))
-    for p in range(3):
-        gathered(p, RING - 1)
-        ka = k[back[p][0]]
-        for d, dl in sides_of:
-            hand(p, 0, sums[p].at[rem4(ka + 2), pl.ds(d * half, half)], fars[p].at[d], dl)
-        for d, dl in sides_of:
-            rows = pl.ds((1 - d) * half, half)
-            hand(p, 1, sums[p].at[rem4(ka + dl + RING), rows], nears[p].at[d, rows], dl)
-    with jax.named_scope("rs1"):
-        for p in range(3):
+    for u in range(2):
+        for p in range(3):
+            cols = piece[p][u]
+            with jax.named_scope("arrive"):
+                got(p, R_B + RING - 1 + u, ms[p].at[pl.ds((RING - 1) * RING, 3), :, :, cols])
+            with jax.named_scope("combine"):
+                combine(p, RING - 1, cols)
             ka = k[back[p][0]]
-            got(p, R_SUM, fars[p])
             for d, dl in sides_of:
-                near = rem4(ka + dl + RING)
-                rows = pl.ds(d * half, half)
-                sums[p][near, rows] = sums[p][near, rows] + fars[p][d]
-                hand(p, 1, sums[p].at[near, rows], nears[p].at[d, rows], dl)
-    with jax.named_scope("rs2"):
-        for p in range(3):
-            got(p, R_SUM + 1, nears[p])
-            out[:, pl.ds(starts[p], widths[p])] = (sums[p][k[back[p][0]]] + nears[p][0] + nears[p][1]).astype(out.dtype)
+                hand(p, u, sums[p].at[rem4(ka + 2), pl.ds(d * half, half), cols], fars[p].at[d, :, cols], dl)
+            for d, dl in sides_of:
+                rows = pl.ds((1 - d) * half, half)
+                hand(p, 2 + u, sums[p].at[rem4(ka + dl + RING), rows, cols], nears[p].at[d, rows, cols], dl)
+    for u in range(2):
+        with jax.named_scope("rs1"):
+            for p in range(3):
+                cols = piece[p][u]
+                ka = k[back[p][0]]
+                got(p, R_SUM + u, fars[p].at[:, :, cols])
+                for d, dl in sides_of:
+                    near = rem4(ka + dl + RING)
+                    rows = pl.ds(d * half, half)
+                    sums[p][near, rows, cols] = sums[p][near, rows, cols] + fars[p][d, :, cols]
+                    hand(p, 2 + u, sums[p].at[near, rows, cols], nears[p].at[d, rows, cols], dl)
+    for u in range(2):
+        with jax.named_scope("rs2"):
+            for p in range(3):
+                cols = piece[p][u]
+                got(p, R_SUM + 2 + u, nears[p].at[:, :, cols])
+                total = sums[p][k[back[p][0]], :, cols] + nears[p][0, :, cols] + nears[p][1, :, cols]
+                out[:, pl.ds(starts[p] + cols.start, cols.size)] = total.astype(out.dtype)
     with jax.named_scope("drain"):
         for p in range(3):
             to_expert[p].wait_sent()
@@ -430,7 +459,7 @@
 
         summed = pl.pallas_call(
             lambda *refs: layer_kernel(dims, *refs),
-            out_shape=jax.ShapeDtypeStruct((toks, d_model), BF16),
+            out_shape=pltpu.VMEM((toks, d_model), BF16),
             in_specs=[any_spec] * 8,
             out_specs=pl.BlockSpec(memory_space=pltpu.VMEM),
             scratch_shapes=[
@@ -449,11 +478,12 @@
                 *bufs(2, toks // 2, dtype=F32),
                 *bufs(2, toks, dtype=F32),
                 pltpu.VMEM((3, n_blocks * SLOTS, toks), BF16),
-                pltpu.VMEM((3, n_blocks * SLOTS, 1), F32),
+                pltpu.VMEM((n_blocks * SLOTS, 3), F32),
                 pltpu.VMEM((3, top_k, toks), jnp.int32),
                 pltpu.VMEM((top_k, toks), F32),
                 pltpu.SemaphoreType.DMA((3, N_SEND)),
                 pltpu.SemaphoreType.DMA((3, N_RECV)),
+                pltpu.SemaphoreType.DMA((RING,)),
                 pltpu.SemaphoreType.DMA((10,)),
             ],
             compiler_params=pltpu.CompilerParams(collective_id=0, has_side_effects=True, vmem_limit_bytes=VMEM_CAP),

time: 150 us -> 146 us (0.973)
  Pallas kernels: 147 us -> 143 us
    pallas_call x1, Pallas kernels: 147 us -> 143 us  [device_layer(): pl.pallas_call(lambda *refs: layer_kernel(dims, *refs), out_shape=pltpu.V...]
where the time goes in v6:
time: 146 us; the launch traced here: 143 us
  Pallas kernels  143 us (98%)
    pallas_call x1, Pallas kernels, device_layer(): pl.pallas_call(lambda *refs: layer_kernel(dims, *refs), out_shape=pltpu.V...  143 us

profile of v6, /device:TPU:1, one launch (start us, length us, event | category | flops | bytes accessed | tf_op | source)
XLA Modules:
  0.0 143.4 jit_solution(375297532246219171)
XLA Ops:
  0.0 142.6 %moe_layer.1 = bf16[128,2048]{1,0:T(8,128)(2,1)S(1)} custom-call(bf16[8,16,2048]{2,1,0:T(8,128)(2,1)} %bitcast.5, s32[8,128]{1,0:T(8,128)} %bitcast.6, s32[8,128]{1,0:T(8,128)} %bitcast.7, s32[8,128]{1,0:T(8,128)} %bitcast.8, f32[8,128]{1,0:T(8,128)} %bitcast.9, bf16[1,2048,768]{2,1,0:T(8,128)(2,1)} %refs_5_.1, bf16[1,2048,768]{2,1,0:T(8,128)(2,1)} %refs_6_.1, ...), custom_call_target="tpu_custom_call" | custom-call | tf_op jit(solution)/shard_map/moe_layer/pallas_call | solution.py:460
  142.6 0.8 copy.10

commit v7 on v6

--- a/solution.py
+++ b/solution.py
@@ -9,7 +9,7 @@
 RING = 4
 SLOTS = 16
 STEPS = (2, 1, -1)
-VMEM_CAP = 65930000
+VMEM_CAP = 66400000
 BF16 = jnp.bfloat16
 F32 = jnp.float32
 
@@ -22,11 +22,15 @@
     def __init__(self):
         self.me = lax.axis_index("expert")
         self.core = lax.rem(self.me, 2)
-        self.k = [rem4(lax.div(self.me, s)) for s in STRIDE]
+        self.grid = [rem4(lax.div(self.me, s)) for s in STRIDE]
+        self.k, self.stride = self.turned(self.grid), self.turned(STRIDE)
+
+    def turned(self, of):
+        return [of[i] + self.core * (of[(i + 1) % 3] - of[i]) for i in range(3)]
 
     def peer(self, axis, delta, core=None):
         there = rem4(self.k[axis] + delta + RING)
-        dev = self.me + (there - self.k[axis]) * STRIDE[axis]
+        dev = self.me + (there - self.k[axis]) * self.stride[axis]
         return dev if core is None else dev + core - self.core
 
     def partner(self):
@@ -50,12 +54,23 @@
 
 
 class Exchange:
-    def __init__(self, pc, c, block, land, send, recv, base):
+    def __init__(self, pc, c, block, land, send, recv, base, by_target=False):
         self.pc, self.c, self.block, self.land = pc, c, block, land
         self.send, self.recv, self.base = send, recv, base
+        ours = pc.k[c], pc.stride[c]
+        if by_target:
+            turn = [(c + core) % 3 for core in range(2)]
+            self.ring = [(pc.grid[ax], STRIDE[ax]) for ax in turn]
+            self.beside = pc.grid[turn[1]] + pc.core * (pc.grid[turn[0]] - pc.grid[turn[1]])
+        else:
+            self.ring = [ours, ours]
+            self.beside = pc.k[c]
+
+    def slot(self, j, at):
+        return j * 8 + at * 2 + self.pc.core
 
     def own(self, j):
-        return j * 8 + self.pc.k[self.c] * 2 + self.pc.core
+        return self.slot(j, self.pc.k[self.c])
 
     def far(self, j):
         return self.to_ring(j, 2)
@@ -63,16 +78,18 @@
     def near(self, j):
         pc = self.pc
         sems = self.send, self.recv.at[self.base + j]
-        across = remote(self.block(j * 8 + pc.k[self.c] * 2 + 1 - pc.core), self.land.at[self.own(j)], *sems, pc.partner())
+        across = remote(self.block(j * 8 + self.beside * 2 + 1 - pc.core), self.land.at[self.slot(j, self.beside)], *sems, pc.partner())
         return self.to_ring(j, 1) + self.to_ring(j, -1) + [across]
 
     def to_ring(self, j, dl):
-        pc, c = self.pc, self.c
-        there = rem4(pc.k[c] + dl + RING)
+        pc = self.pc
         sems = self.send, self.recv.at[self.base + j]
-        return [
-            remote(self.block(j * 8 + there * 2 + core), self.land.at[self.own(j)], *sems, pc.peer(c, dl, core)) for core in range(2)
-        ]
+        out = []
+        for core, (at, stride) in enumerate(self.ring):
+            there = rem4(at + dl + RING)
+            dev = pc.me + (there - at) * stride + core - pc.core
+            out.append(remote(self.block(j * 8 + there * 2 + core), self.land.at[self.slot(j, at)], *sems, dev))
+        return out
 
     def sends(self, j):
         return self.far(j) + self.near(j)
@@ -174,8 +191,8 @@
         a, b, c = axes[p]
         aa, bb = rem4(k[a] + da), rem4(k[b] + db)
         j = rem4(aa + bb + k[c])
-        first = SLOTS * (pc.me - k[c] * STRIDE[c] - pc.core)
-        rows = (first + (row >> 5) * (SLOTS * STRIDE[c]) + (row & 31)).astype(F32)
+        first = SLOTS * (pc.me - k[c] * pc.stride[c] - pc.core)
+        rows = (first + (row >> 5) * (SLOTS * pc.stride[c]) + (row & 31)).astype(F32)
         ids = mm[p, bb, aa][:top_k]
         chosen = sum(jnp.where(hit, 1.0, 0.0) for hit in slots_of(rows, ids)).astype(BF16)
         block = ts[p][pl.ds((bb * RING + aa) * 8, 8)].reshape(toks, widths[p])
@@ -253,7 +270,7 @@
         for p in range(3):
             sides(p, 2)
     to_source = [
-        Exchange(pc, back[p][2], (lambda n, p=p: ts[p].at[pl.ds(n * RING, RING)]), cs[p], send.at[p, S_BACK], recv.at[p], R_BACK)
+        Exchange(pc, back[p][2], (lambda n, p=p: ts[p].at[pl.ds(n * RING, RING)]), cs[p], send.at[p, S_BACK], recv.at[p], R_BACK, True)
         for p in range(3)
     ]
 
@@ -287,6 +304,30 @@
 
                     offer(p, j, far=False)
 
+    def prepare(p, j, bank):
+        a, b, c = back[p]
+        src = rem4(j + 2 * RING - k[c] - k[b])
+        first = SLOTS * (pc.me - k[b] * pc.stride[b] - k[c] * pc.stride[c] - pc.core)
+        info = mm[(p + 2) % 3, k[b], src]
+        rows = first + (row >> 5) * (SLOTS * pc.stride[c]) + (row & 31)
+
+        @pl.loop(0, RING)
+        def _(bb):
+            hits = slots_of((rows + bb * (SLOTS * pc.stride[b])).astype(F32), info[:top_k])
+            chosen = sum(jnp.where(hit, 1.0, 0.0) for hit in hits)
+            gate = sum(jnp.where(hit, info[top_k + n:top_k + n + 1, :], 0.0) for n, hit in enumerate(hits))
+            at = pl.ds(pl.multiple_of(bb * 8 * SLOTS, 8 * SLOTS), 8 * SLOTS)
+            hot[bank, p, at] = chosen.astype(BF16)
+            scale[at, 3 * bank + p:3 * bank + p + 1] = jnp.sum(gate, axis=1, keepdims=True)
+
+    def prepared(j, bank):
+        with jax.named_scope("prepare"):
+            for p in range(3):
+                prepare(p, j, bank)
+
+    prepared(RING - 1, 1)
+    prepared(0, 0)
+
     for cp in weights:
         cp.wait()
     for p in range(3):
@@ -297,7 +338,7 @@
     def places(order, j, zy, core):
         z, yy = lax.div(zy, RING), rem4(zy)
         at = (z, yy, rem4(j + 2 * RING - z - yy))
-        return [(j * 8 + at[c] * 2 + core, at[b]) for a, b, c in order]
+        return [(j * 8 + at[(c + core) % 3] * 2 + core, at[(b + core) % 3]) for a, b, c in order]
 
     def ffn(j):
         @pl.loop(0, RING * RING)
@@ -352,23 +393,7 @@
             kb = k[back[p][1]]
             ms[p][j * RING + kb] = cs[p][pl.ds(j * 8, 8), kb]
 
-    def prepare(p, j):
-        a, b, c = back[p]
-        src = rem4(j + 2 * RING - k[c] - k[b])
-        first = SLOTS * (pc.me - k[b] * STRIDE[b] - k[c] * STRIDE[c] - pc.core)
-        info = mm[(p + 2) % 3, k[b], src]
-        rows = first + (row >> 5) * (SLOTS * STRIDE[c]) + (row & 31)
-
-        @pl.loop(0, RING)
-        def _(bb):
-            hits = slots_of((rows + bb * (SLOTS * STRIDE[b])).astype(F32), info[:top_k])
-            chosen = sum(jnp.where(hit, 1.0, 0.0) for hit in hits)
-            gate = sum(jnp.where(hit, info[top_k + n:top_k + n + 1, :], 0.0) for n, hit in enumerate(hits))
-            at = pl.ds(pl.multiple_of(bb * 8 * SLOTS, 8 * SLOTS), 8 * SLOTS)
-            hot[p, at] = chosen.astype(BF16)
-            scale[at, p:p + 1] = jnp.sum(gate, axis=1, keepdims=True)
-
-    def combine(p, j, cols):
+    def combine(p, j, cols, bank):
         a, b, c = back[p]
         src = rem4(j + 2 * RING - k[c] - k[b])
         xcols = pl.ds(starts[p] + cols.start, cols.size)
@@ -377,25 +402,22 @@
         def _(bb):
             at = pl.ds(pl.multiple_of(bb * 8 * SLOTS, 8 * SLOTS), 8 * SLOTS)
             rows = ms[p][j * RING + bb, :, :, cols].reshape(8 * SLOTS, cols.size)
-            x[at, xcols] = (rows.astype(F32) * scale[at, p:p + 1]).astype(BF16)
-
-        sums[p][src, :, cols] = lax.dot_general(hot[p], x[:, xcols], (((0,), (0,)), ((), ())), preferred_element_type=F32)
-
-    def prepared(j):
-        with jax.named_scope("prepare"):
-            for p in range(3):
-                prepare(p, j)
+            x[at, xcols] = (rows.astype(F32) * scale[at, 3 * bank + p:3 * bank + p + 1]).astype(BF16)
+
+        sums[p][src, :, cols] = lax.dot_general(hot[bank, p], x[:, xcols], (((0,), (0,)), ((), ())), preferred_element_type=F32)
 
     @pl.loop(0, RING - 1)
     def _(j):
-        prepared(j)
         for p in range(3):
             with jax.named_scope("arrive"):
                 got(p, R_B + j, ms[p].at[pl.ds(j * RING, 3)])
             with jax.named_scope("combine"):
-                combine(p, j, pl.ds(0, widths[p]))
-
-    prepared(RING - 1)
+                combine(p, j, pl.ds(0, widths[p]), 0)
+
+        @pl.when(j < RING - 2)
+        def _():
+            prepared(j + 1, 0)
+
 
     def hand(p, r, ref, dst, dl):
         remote(ref, dst, send.at[p, S_SUM], recv.at[p, R_SUM + r], pc.peer(back[p][0], dl)).start()
@@ -407,7 +429,7 @@
             with jax.named_scope("arrive"):
                 got(p, R_B + RING - 1 + u, ms[p].at[pl.ds((RING - 1) * RING, 3), :, :, cols])
             with jax.named_scope("combine"):
-                combine(p, RING - 1, cols)
+                combine(p, RING - 1, cols, 1)
             ka = k[back[p][0]]
             for d, dl in sides_of:
                 hand(p, u, sums[p].at[rem4(ka + 2), pl.ds(d * half, half), cols], fars[p].at[d, :, cols], dl)
@@ -477,8 +499,8 @@
                 *bufs(RING, toks, dtype=F32),
                 *bufs(2, toks // 2, dtype=F32),
                 *bufs(2, toks, dtype=F32),
-                pltpu.VMEM((3, n_blocks * SLOTS, toks), BF16),
-                pltpu.VMEM((n_blocks * SLOTS, 3), F32),
+                pltpu.VMEM((2, 3, n_blocks * SLOTS, toks), BF16),
+                pltpu.VMEM((n_blocks * SLOTS, 6), F32),
                 pltpu.VMEM((3, top_k, toks), jnp.int32),
                 pltpu.VMEM((top_k, toks), F32),
                 pltpu.SemaphoreType.DMA((3, N_SEND)),

time: 146 us -> 145 us (level); the launches traced: 143 us -> 144 us
  no operation moved by 1% of the time
where the time goes in v7:
time: 145 us; the launch traced here: 144 us
  Pallas kernels  144 us (99%)
    pallas_call x1, Pallas kernels, device_layer(): pl.pallas_call(lambda *refs: layer_kernel(dims, *refs), out_shape=pltpu.V...  144 us

profile of v7, /device:TPU:1, one launch (start us, length us, event | category | flops | bytes accessed | tf_op | source)
XLA Modules:
  0.0 144.4 jit_solution(6937647438038322906)
XLA Ops:
  0.0 143.6 %moe_layer.1 = bf16[128,2048]{1,0:T(8,128)(2,1)S(1)} custom-call(bf16[8,16,2048]{2,1,0:T(8,128)(2,1)} %bitcast.5, s32[8,128]{1,0:T(8,128)} %bitcast.6, s32[8,128]{1,0:T(8,128)} %bitcast.7, s32[8,128]{1,0:T(8,128)} %bitcast.8, f32[8,128]{1,0:T(8,128)} %bitcast.9, bf16[1,2048,768]{2,1,0:T(8,128)(2,1)} %refs_5_.1, bf16[1,2048,768]{2,1,0:T(8,128)(2,1)} %refs_6_.1, ...), custom_call_target="tpu_custom_call" | custom-call | tf_op jit(solution)/shard_map/moe_layer/pallas_call | solution.py:482
  143.6 0.8 copy.10

commit v8 on v7

--- a/solution.py
+++ b/solution.py
@@ -193,7 +193,7 @@
         j = rem4(aa + bb + k[c])
         first = SLOTS * (pc.me - k[c] * pc.stride[c] - pc.core)
         rows = (first + (row >> 5) * (SLOTS * pc.stride[c]) + (row & 31)).astype(F32)
-        ids = mm[p, bb, aa][:top_k]
+        ids = mm[p, bb, aa, pl.ds(0, top_k)]
         chosen = sum(jnp.where(hit, 1.0, 0.0) for hit in slots_of(rows, ids)).astype(BF16)
         block = ts[p][pl.ds((bb * RING + aa) * 8, 8)].reshape(toks, widths[p])
         picked = jnp.dot(chosen, block, preferred_element_type=F32).astype(BF16)
@@ -227,7 +227,7 @@
         for p in range(3):
             got(p, R_META, mm.at[p, 0, pl.ds(0, 3)])
             for dl in STEPS:
-                push(p, S_META + 1, R_META + 1, mm.at[p, k[axes[p][1]]], pc.peer(axes[p][1], dl))
+                push(p, S_META + 1, R_META + 1, mm.at[p, k[axes[p][1]], :, pl.ds(0, top_k)], pc.peer(axes[p][1], dl))
     with jax.named_scope("ag_a"):
         for p in range(3):
             got(p, R_A, blk(p, 3, 0))
@@ -251,7 +251,7 @@
         for p in range(3):
             b_sides(p, 0)
     for p in range(3):
-        got(p, R_META + 1, mm.at[p, pl.ds(0, 3)])
+        got(p, R_META + 1, mm.at[p, pl.ds(0, 3), :, pl.ds(0, top_k)])
     with jax.named_scope("pick1"):
         for p in range(3):
             pick(p, 2, 0)
@@ -332,7 +332,7 @@
         cp.wait()
     for p in range(3):
         gone(p, S_META, mm.at[p, 0, pl.ds(0, 3)])
-        gone(p, S_META + 1, mm.at[p, pl.ds(0, 3)])
+        gone(p, S_META + 1, mm.at[p, pl.ds(0, 3), :, pl.ds(0, top_k)])
         gone(p, S_GATHER, some(p, 15))
 
     def places(order, j, zy, core):

time: 145 us -> 144 us (level)
  no operation moved by 1% of the time
where the time goes in v8:
time: 144 us
  Pallas kernels  143 us (99%)
    pallas_call x1, Pallas kernels, device_layer(): pl.pallas_call(lambda *refs: layer_kernel(dims, *refs), out_shape=pltpu.V...  143 us

profile of v8, /device:TPU:1, one launch (start us, length us, event | category | flops | bytes accessed | tf_op | source)
XLA Modules:
  0.0 143.7 jit_solution(13323859417901758590)
XLA Ops:
  0.0 142.9 %moe_layer.1 = bf16[128,2048]{1,0:T(8,128)(2,1)S(1)} custom-call(bf16[8,16,2048]{2,1,0:T(8,128)(2,1)} %bitcast.5, s32[8,128]{1,0:T(8,128)} %bitcast.6, s32[8,128]{1,0:T(8,128)} %bitcast.7, s32[8,128]{1,0:T(8,128)} %bitcast.8, f32[8,128]{1,0:T(8,128)} %bitcast.9, bf16[1,2048,768]{2,1,0:T(8,128)(2,1)} %refs_5_.1, bf16[1,2048,768]{2,1,0:T(8,128)(2,1)} %refs_6_.1, ...), custom_call_target="tpu_custom_call" | custom-call | tf_op jit(solution)/shard_map/moe_layer/pallas_call | solution.py:482
  142.9 0.8 copy.10

commit v9 on v8

--- a/solution.py
+++ b/solution.py
@@ -136,25 +136,25 @@
         return ts[p].at[pl.ds(spot(p, da, db) * 8 + d * 4, 4)]
 
     loads = [
-        pltpu.make_async_copy(tok.at[:, :, pl.ds(starts[p], widths[p])], blk(p, 0, 0), here.at[p]) for p in range(3)
+        pltpu.make_async_copy(tok.at[:, :, pl.ds(starts[p], widths[p])], blk(p, 0, 0), here.at[0]) for p in range(3)
     ]
-    routes = [pltpu.make_async_copy(src, raw.at[n], here.at[6 + n]) for n, src in enumerate((ids, devs, exps))]
-    routes.append(pltpu.make_async_copy(gates, hot_gate, here.at[9]))
-    weights = [pltpu.make_async_copy(src.at[0], dst, here.at[3 + n]) for n, (src, dst) in enumerate(((wg, vg), (wu, vu), (wd, vd)))]
+    routes = [pltpu.make_async_copy(src, raw.at[n], here.at[4]) for n, src in enumerate((ids, devs, exps))]
+    routes.append(pltpu.make_async_copy(gates, hot_gate, here.at[4]))
+    weights = [pltpu.make_async_copy(src.at[0], dst, here.at[1 + n]) for n, (src, dst) in enumerate(((wg, vg), (wu, vu), (wd, vd)))]
     for cp in routes + loads:
         cp.start()
     with jax.named_scope("barrier"):
         pc.greet()
-        for cp in routes:
-            cp.wait()
+        four = mm.at[0, 0, pl.ds(0, 2)]
+        pltpu.make_async_copy(four, four, here.at[4]).wait()
         kept = (raw[1] >= 0) & (raw[2] >= 0)
         dest = jnp.where(kept, raw[0] * SLOTS + raw[1], -1).astype(F32)
         gate_bf = hot_gate[...].astype(BF16).astype(F32)
         for p, (a, b, c) in enumerate(axes):
             mm[p, k[b], k[a], pl.ds(0, top_k)] = dest
             mm[p, k[b], k[a], pl.ds(top_k, top_k)] = gate_bf
-        for cp in loads:
-            cp.wait()
+        mine = x.at[pl.ds(0, toks)]
+        pltpu.make_async_copy(mine, mine, here.at[0]).wait()
         pc.meet()
 
     def push(p, s, r, ref, dev):
@@ -506,7 +506,7 @@
                 pltpu.SemaphoreType.DMA((3, N_SEND)),
                 pltpu.SemaphoreType.DMA((3, N_RECV)),
                 pltpu.SemaphoreType.DMA((RING,)),
-                pltpu.SemaphoreType.DMA((10,)),
+                pltpu.SemaphoreType.DMA((5,)),
             ],
             compiler_params=pltpu.CompilerParams(collective_id=0, has_side_effects=True, vmem_limit_bytes=VMEM_CAP),
             name="moe_layer",

time: 144 us -> 144 us (level)
  no operation moved by 1% of the time
where the time goes in v9:
time: 144 us
  Pallas kernels  143 us (99%)
    pallas_call x1, Pallas kernels, device_layer(): pl.pallas_call(lambda *refs: layer_kernel(dims, *refs), out_shape=pltpu.V...  143 us

profile of v9, /device:TPU:1, one launch (start us, length us, event | category | flops | bytes accessed | tf_op | source)
XLA Modules:
  0.0 143.7 jit_solution(13890551616137857607)
XLA Ops:
  0.0 142.9 %moe_layer.1 = bf16[128,2048]{1,0:T(8,128)(2,1)S(1)} custom-call(bf16[8,16,2048]{2,1,0:T(8,128)(2,1)} %bitcast.5, s32[8,128]{1,0:T(8,128)} %bitcast.6, s32[8,128]{1,0:T(8,128)} %bitcast.7, s32[8,128]{1,0:T(8,128)} %bitcast.8, f32[8,128]{1,0:T(8,128)} %bitcast.9, bf16[1,2048,768]{2,1,0:T(8,128)(2,1)} %refs_5_.1, bf16[1,2048,768]{2,1,0:T(8,128)(2,1)} %refs_6_.1, ...), custom_call_target="tpu_custom_call" | custom-call | tf_op jit(solution)/shard_map/moe_layer/pallas_call | solution.py:482
  142.9 0.8 copy.10
